TPU v7x, 32 devices: a whole 2x2x4 slice. The times are simulated.
32 devices in a mesh: groups: 2 (over y), ctx: 4 (over z), tp: 4 (over x, core).
Axes of the slice: x: 2, y: 2, z: 4, core: 2. Of those that a mesh axis runs over, the one named last changes fastest.
Arguments:
- query_matrix: bfloat16 [1024, 8192], P(('groups', 'ctx'), 'tp'), parts along dimension 0, may hold values from -20 to 20
- key_matrix: bfloat16 [1024, 1024], P(('groups', 'ctx'), 'tp'), parts along dimension 0, may hold values from -20 to 20
- value_matrix: bfloat16 [1024, 1024], P(('groups', 'ctx'), 'tp'), parts along dimension 0, may hold values from -6 to 6
- doc_ids: int32 [1024], P('groups'), parts along dimension 0, may hold values from 0 to 5, never falling along the last dimension, each value on 1 to 256 neighbouring positions
- out_weight: bfloat16 [8192, 4096], P('tp', 'ctx'), may hold values from -0.0625 to 0.0625
Outputs:
- projected: bfloat16 [1024, 4096], P(('groups', 'ctx'), 'tp'), parts along dimension 0
There are 2 independent parts, one for each index of `groups`. A program takes and returns all parts, laid end to end along the dimension named above; an argument that names none is the same for every part. Nothing has to cross between parts.
Inputs may be any that keep to these rules, and one draw needn't show every extreme that they name: `doc_ids`: non-decreasing along the sequence; each document holds 1 to 256 tokens, one exactly 256.
All inputs are finite; a program needn't handle non-finite values.
Results may differ from a plain program's by a relative error of at most 0.015.
Values may be sent and summed in bfloat16 or wider, within the bound.
A program may use at most 64 MiB of HBM per device.

v0:
```python
import functools
import math

import jax
import jax.numpy as jnp
import numpy as np
from jax import lax
from jax.experimental import pallas as pl
from jax.experimental.pallas import tpu as pltpu
from jax.sharding import PartitionSpec as P

MESH = pl.DeviceIdType.MESH

HEAD_SIZE = 128


rope_base = 1000000.0


def rotary_tables(rows, token_positions, heads):
    half_dim = HEAD_SIZE // 2
    frequency = jnp.power(
        jnp.float32(rope_base), -jnp.arange(half_dim, dtype=jnp.float32) * (2.0 / HEAD_SIZE)
    )
    angles = token_positions.astype(jnp.float32)[:, None] * frequency[None, :]
    cosine = jnp.cos(angles)[:, None, :]
    sine = jnp.sin(angles)[:, None, :]
    values = rows.astype(jnp.float32).reshape(rows.shape[0], heads, HEAD_SIZE)
    first = values[..., :half_dim]
    second = values[..., half_dim:]
    turned = jnp.concatenate([first * cosine - second * sine, second * cosine + first * sine], -1)
    return turned.reshape(rows.shape[0], heads * HEAD_SIZE).astype(jnp.bfloat16)


def on_device(query_matrix, key_matrix, value_matrix, doc_ids, out_weight):
    ctx_index = lax.axis_index("ctx")
    tok_rows = query_matrix.shape[0]
    query_heads = query_matrix.shape[1] // HEAD_SIZE
    key_heads = key_matrix.shape[1] // HEAD_SIZE
    group_width = query_heads // key_heads
    inverse_root = HEAD_SIZE ** (-0.5)
    local_rows = jnp.arange(tok_rows, dtype=jnp.int32)
    given_pos = ctx_index * tok_rows + local_rows
    query_matrix_rot = rotary_tables(query_matrix, given_pos, query_heads)
    keys_here = rotary_tables(key_matrix, given_pos, key_heads)
    query_doc = jnp.take(doc_ids, given_pos, axis=0)
    query_four = query_matrix_rot.reshape(tok_rows, key_heads, group_width, HEAD_SIZE)

    def attend(state, block):
        key_block, value_block, doc_block, pos_block = block
        row_max, totals, accum = state
        scores = (
            jnp.einsum("qkgd,skd->kgqs", query_four, key_block, preferred_element_type=jnp.float32)
            * inverse_root
        )
        allowed = (
            (query_doc[:, None] == doc_block[None, :]) & (pos_block[None, :] <= given_pos[:, None])
        )[None, None]
        new_max = jnp.maximum(row_max, jnp.max(jnp.where(allowed, scores, -1e30), -1))
        weights = jnp.where(allowed, jnp.exp(scores - new_max[..., None]), 0.0)
        factor = jnp.exp(row_max - new_max)
        totals = totals * factor + jnp.sum(weights, -1)
        accum = accum * jnp.transpose(factor, (2, 0, 1))[..., None] + jnp.einsum(
            "kgqs,skd->qkgd",
            weights.astype(jnp.bfloat16),
            value_block,
            preferred_element_type=jnp.float32,
        )
        return (new_max, totals, accum)

    start_state = (
        jnp.full((key_heads, group_width, tok_rows), -1e30, jnp.float32),
        jnp.zeros((key_heads, group_width, tok_rows), jnp.float32),
        jnp.zeros((tok_rows, key_heads, group_width, HEAD_SIZE), jnp.float32),
    )
    key_piece = lax.all_gather(keys_here, "ctx", axis=0, tiled=True)
    value_piece = lax.all_gather(value_matrix, "ctx", axis=0, tiled=True)
    count = key_piece.shape[0]
    block_rows = math.gcd(count, 512)
    block_count = count // block_rows
    positions = jnp.arange(count, dtype=jnp.int32)
    blocks = (
        key_piece.reshape(block_count, block_rows, key_heads, HEAD_SIZE),
        value_piece.reshape(block_count, block_rows, key_heads, HEAD_SIZE),
        jnp.take(doc_ids, positions, axis=0).reshape(block_count, block_rows),
        positions.reshape(block_count, block_rows),
    )

    def step_block(inner_state, block):
        return (attend(inner_state, block), None)

    final_state, unused_out = lax.scan(step_block, start_state, blocks)
    row_max, totals, accum = final_state
    attention = (
        (accum / jnp.transpose(totals, (2, 0, 1))[..., None])
        .reshape(tok_rows, query_heads * HEAD_SIZE)
        .astype(jnp.bfloat16)
    )
    terms = jnp.dot(
        attention,
        lax.all_gather(out_weight, "ctx", axis=1, tiled=True),
        preferred_element_type=jnp.float32,
    )
    return lax.psum_scatter(terms.astype(jnp.bfloat16), "tp", scatter_dimension=1, tiled=True)


def fused_kernel(
    n, back, query_ref, key_ref, value_ref, doc_ref, table_ref, weight_ref, out_ref,
    query_in, key_in, table, docs, weight, rotated, bias, kv, gathered, total_lo, total_hi,
    partial, quarters, summed, landed,
    load_sem, weight_sem, kv_send, kv_recv, up_send, down_send, chunk_recv,
    quarter_send, quarter_recv, result_send, result_recv, store_sem,
):
    ctx = lax.axis_index("ctx")
    tp = lax.axis_index("tp")
    rows = query_ref.shape[0]
    kv_heads = key_ref.shape[1] // HEAD_SIZE
    query_heads = query_ref.shape[1] // HEAD_SIZE
    group_width = query_heads // kv_heads
    chunks = gathered.shape[1]
    chunk_width = gathered.shape[3]
    chunk_heads = chunk_width // HEAD_SIZE
    quarter = partial.shape[3]
    last = n - 1

    def remote(src, dst, send, recv, to_ctx, to_tp):
        return pltpu.make_async_remote_copy(
            src_ref=src, dst_ref=dst, send_sem=send, recv_sem=recv,
            device_id={"ctx": to_ctx, "tp": to_tp}, device_id_type=MESH,
        )

    barrier = pltpu.get_barrier_semaphore()
    for step in range(1, n * n):
        pl.semaphore_signal(
            barrier, inc=1,
            device_id={"ctx": lax.rem(ctx + step // n, n), "tp": lax.rem(tp + step % n, n)},
            device_id_type=MESH,
        )

    first_row = pl.multiple_of(ctx * rows, rows)
    loads = [
        pltpu.make_async_copy(key_ref, key_in, load_sem.at[0]),
        pltpu.make_async_copy(table_ref.at[:, pl.ds(first_row, rows)], table, load_sem.at[1]),
        pltpu.make_async_copy(doc_ref, docs, load_sem.at[2]),
        pltpu.make_async_copy(query_ref, query_in, load_sem.at[3]),
    ]
    value_loads = [
        pltpu.make_async_copy(
            value_ref.at[:, pl.ds(head * HEAD_SIZE, HEAD_SIZE)], kv.at[back, head, 1], load_sem.at[4 + head]
        )
        for head in range(kv_heads)
    ]
    weight_loads = [
        pltpu.make_async_copy(
            weight_ref.at[pl.ds(chunk * chunk_width, chunk_width)], weight.at[chunk], weight_sem.at[chunk]
        )
        for chunk in range(chunks)
    ]
    for load in loads + value_loads + weight_loads:
        load.start()

    def turn(values):
        values = values.astype(jnp.float32)
        return (values * table[0] + pltpu.roll(values, HEAD_SIZE // 2, 1) * table[1]).astype(jnp.bfloat16)

    loads[0].wait()
    loads[1].wait()
    for head in range(kv_heads):
        kv[back, head, 0] = turn(key_in[:, head * HEAD_SIZE : (head + 1) * HEAD_SIZE])
    for load in value_loads:
        load.wait()

    for slot in range(back):
        @pl.when(ctx < back - slot)
        def _():
            kv[slot] = jnp.zeros(kv.shape[1:], kv.dtype)

    pl.semaphore_wait(barrier, n * n - 1)

    def kv_copy(slot, head):
        return remote(
            kv.at[slot, head], kv.at[slot - 1, head], kv_send.at[slot, head], kv_recv.at[slot - 1, head],
            lax.rem(ctx + 1, n), tp,
        )

    def kv_sends(slot):
        return (ctx < last) & (ctx >= back - slot)

    @pl.when(ctx < last)
    def _():
        for head in range(kv_heads):
            kv_copy(back, head).start()

    loads[2].wait()
    own_docs = jnp.broadcast_to(docs[pl.ds(ctx, 1), :], (rows, rows)).astype(jnp.float32).T
    row_index = lax.broadcasted_iota(jnp.int32, (rows, rows), 0)
    column_index = lax.broadcasted_iota(jnp.int32, (rows, rows), 1)
    for slot in range(back + 1):
        block = ctx - back + slot
        their_docs = docs[pl.ds(lax.max(block, 0), 1), :].astype(jnp.float32)
        allowed = (own_docs == their_docs) & (block * rows + column_index <= ctx * rows + row_index) & (block >= 0)
        bias[slot] = jnp.where(allowed, 0.0, -1e30)

    loads[3].wait()
    for head in range(query_heads):
        rotated[head] = turn(query_in[:, head * HEAD_SIZE : (head + 1) * HEAD_SIZE])

    for slot in range(back - 1, 0, -1):
        for head in range(kv_heads):
            @pl.when(ctx >= back - slot)
            def _():
                kv_copy(slot + 1, head).wait_recv()

            @pl.when(kv_sends(slot))
            def _():
                kv_copy(slot, head).start()

    def up_copy(block, chunk):
        here = gathered.at[block, chunk]
        return remote(here, here, up_send.at[block, chunk], chunk_recv.at[block, chunk], lax.rem(ctx + 1, n), tp)

    def down_copy(block, chunk):
        here = gathered.at[block, chunk]
        return remote(here, here, down_send.at[block, chunk], chunk_recv.at[block, chunk], lax.rem(ctx + last, n), tp)

    scale = HEAD_SIZE ** (-0.5) * math.log2(math.e)
    contract = (((1,), (1,)), ((), ()))
    for head in range(query_heads):
        kv_head = head // group_width
        if head % group_width == 0:
            @pl.when(ctx >= back)
            def _():
                kv_copy(1, kv_head).wait_recv()

        scores = [
            lax.dot_general(rotated[head], kv[slot, kv_head, 0], contract, preferred_element_type=jnp.float32) * scale
            + bias[slot]
            for slot in range(back + 1)
        ]
        row_max = functools.reduce(jnp.maximum, scores).max(-1, keepdims=True)
        weights = [jnp.exp2(score - row_max) for score in scores]
        totals = sum(weights).sum(-1, keepdims=True)
        mixed = sum(
            jnp.dot(weights[slot].astype(jnp.bfloat16), kv[slot, kv_head, 1], preferred_element_type=jnp.float32)
            for slot in range(back + 1)
        )
        chunk, place = head // chunk_heads, head % chunk_heads
        gathered[ctx, chunk, :, place * HEAD_SIZE : (place + 1) * HEAD_SIZE] = (mixed / totals).astype(jnp.bfloat16)
        if place == chunk_heads - 1:
            @pl.when(ctx < last)
            def _():
                up_copy(ctx, chunk).start()

            @pl.when(ctx > 0)
            def _():
                down_copy(ctx, chunk).start()

    def quarter_copy(block, hop):
        to = lax.rem(tp + hop, n)
        return remote(
            partial.at[block, to], quarters.at[block, hop], quarter_send.at[block, hop], quarter_recv.at[block, hop],
            ctx, to,
        )

    def project(block, chunk, total):
        for hop in list(range(1, n)) + [0]:
            part = lax.rem(tp + hop, n)
            columns = pl.ds(pl.multiple_of(part * quarter, quarter), quarter)
            product = jnp.dot(
                gathered[block, chunk], weight[chunk, :, columns], preferred_element_type=jnp.float32
            )
            if chunk > 0:
                product = product + total[hop]
            if chunk < chunks - 1:
                total[hop] = product
            else:
                partial[block, part] = product.astype(jnp.bfloat16)
                if hop:
                    quarter_copy(block, hop).start()

    def result_copy(block):
        return remote(
            summed.at[block], landed.at[tp], result_send.at[block], result_recv.at[tp], block, ctx
        )

    def finish(block):
        value = partial[block, tp].astype(jnp.float32)
        for hop in range(1, n):
            quarter_copy(block, hop).wait_recv()
            value = value + quarters[block, hop].astype(jnp.float32)
        value = value.astype(jnp.bfloat16)
        mine = (block == ctx) & (tp == ctx)

        @pl.when(mine)
        def _():
            landed[tp] = value

        @pl.when(jnp.logical_not(mine))
        def _():
            summed[block] = value
            result_copy(block).start()

    for load in weight_loads:
        load.wait()
    for chunk in range(chunks):
        project(ctx, chunk, total_lo)

    def finish_pair(step):
        @pl.when(ctx - step >= 0)
        def _():
            finish(lax.max(ctx - step, 0))

        @pl.when((ctx + step <= last) & (step > 0))
        def _():
            finish(lax.min(ctx + step, last))

    def gather_step(step, carry):
        low, high = lax.max(ctx - step, 0), lax.min(ctx + step, last)
        has_low, has_high = ctx - step >= 0, ctx + step <= last
        for chunk in range(chunks):
            @pl.when(has_low)
            def _():
                up_copy(low, chunk).wait_recv()

                @pl.when(ctx < last)
                def _():
                    up_copy(low, chunk).start()

            @pl.when(has_high)
            def _():
                down_copy(high, chunk).wait_recv()

                @pl.when(ctx > 0)
                def _():
                    down_copy(high, chunk).start()

            @pl.when(has_low)
            def _():
                project(low, chunk, total_lo)

            @pl.when(has_high)
            def _():
                project(high, chunk, total_hi)

        finish_pair(step - 1)
        return carry

    lax.fori_loop(1, n, gather_step, 0)
    finish_pair(last)

    for part in range(n):
        @pl.when(jnp.logical_not((tp == ctx) & (tp == part)))
        def _():
            remote(
                summed.at[0], landed.at[part], result_send.at[0], result_recv.at[part], ctx, part
            ).wait_recv()

        pltpu.make_async_copy(
            landed.at[part], out_ref.at[:, pl.ds(part * quarter, quarter)], store_sem.at[part]
        ).start()

    for slot in range(1, back + 1):
        for head in range(kv_heads):
            @pl.when(kv_sends(slot))
            def _():
                kv_copy(slot, head).wait_send()

    def drain(block, carry):
        for chunk in range(chunks):
            @pl.when((block <= ctx) & (ctx < last))
            def _():
                up_copy(block, chunk).wait_send()

            @pl.when((block >= ctx) & (ctx > 0))
            def _():
                down_copy(block, chunk).wait_send()

        for hop in range(1, n):
            quarter_copy(block, hop).wait_send()

        @pl.when(jnp.logical_not((block == ctx) & (tp == ctx)))
        def _():
            result_copy(block).wait_send()

        return carry

    lax.fori_loop(0, n, drain, 0)
    for part in range(n):
        pltpu.make_async_copy(
            landed.at[part], out_ref.at[:, pl.ds(part * quarter, quarter)], store_sem.at[part]
        ).wait()


def fused(n, query_matrix, key_matrix, value_matrix, doc_ids, out_weight):
    rows, query_width = query_matrix.shape
    query_heads, kv_heads = query_width // HEAD_SIZE, key_matrix.shape[1] // HEAD_SIZE
    features = out_weight.shape[1]
    tokens = doc_ids.shape[0]
    back = -(-(tokens // 2 - 1) // rows)
    chunks = 4
    chunk_width = query_width // chunks
    quarter = features // n
    half = HEAD_SIZE // 2
    frequency = np.power(np.float32(rope_base), -np.arange(half, dtype=np.float32) * np.float32(2.0 / HEAD_SIZE))
    angles = np.arange(tokens, dtype=np.float32)[:, None] * frequency[None, :]
    cosine, sine = np.cos(angles), np.sin(angles)
    table = np.stack([np.concatenate([cosine, cosine], 1), np.concatenate([-sine, sine], 1)]).astype(np.float32)
    any_space = pl.BlockSpec(memory_space=pl.ANY)
    bf16, f32, dma = jnp.bfloat16, jnp.float32, pltpu.SemaphoreType.DMA
    return pl.pallas_call(
        functools.partial(fused_kernel, n, back),
        out_shape=jax.ShapeDtypeStruct((rows, features), bf16),
        in_specs=[any_space] * 6,
        out_specs=any_space,
        scratch_shapes=[
            pltpu.VMEM((rows, query_width), bf16),
            pltpu.VMEM((rows, kv_heads * HEAD_SIZE), bf16),
            pltpu.VMEM((2, rows, HEAD_SIZE), f32),
            pltpu.VMEM((tokens // rows, rows), jnp.int32),
            pltpu.VMEM((chunks, chunk_width, features), bf16),
            pltpu.VMEM((query_heads, rows, HEAD_SIZE), bf16),
            pltpu.VMEM((back + 1, rows, rows), f32),
            pltpu.VMEM((back + 1, kv_heads, 2, rows, HEAD_SIZE), bf16),
            pltpu.VMEM((n, chunks, rows, chunk_width), bf16),
            pltpu.VMEM((n, rows, quarter), f32),
            pltpu.VMEM((n, rows, quarter), f32),
            pltpu.VMEM((n, n, rows, quarter), bf16),
            pltpu.VMEM((n, n, rows, quarter), bf16),
            pltpu.VMEM((n, rows, quarter), bf16),
            pltpu.VMEM((n, rows, quarter), bf16),
            dma((4 + kv_heads,)),
            dma((chunks,)),
            dma((back + 1, kv_heads)),
            dma((back + 1, kv_heads)),
            dma((n, chunks)),
            dma((n, chunks)),
            dma((n, chunks)),
            dma((n, n)),
            dma((n, n)),
            dma((n,)),
            dma((n,)),
            dma((n,)),
        ],
        compiler_params=pltpu.CompilerParams(collective_id=0, has_side_effects=True),
    )(query_matrix, key_matrix, value_matrix, doc_ids.reshape(tokens // rows, rows), jnp.asarray(table), out_weight)


def solution(mesh):
    in_specs = (
        P(("groups", "ctx"), "tp"),
        P(("groups", "ctx"), "tp"),
        P(("groups", "ctx"), "tp"),
        P("groups"),
        P("tp", "ctx"),
    )
    out_specs = P(("groups", "ctx"), "tp")
    n = mesh.shape["ctx"]
    body = functools.partial(fused, n) if n == mesh.shape["tp"] else on_device
    return jax.shard_map(
        body, mesh=mesh, in_specs=in_specs, out_specs=out_specs, check_vma=False
    )
```

profile of v0, /device:TPU:3, one launch (start us, length us, event | category | flops | bytes accessed | tf_op | source)
XLA Modules:
  0.0 60.1 jit_solution(1360570060710609187)
XLA Ops:
  0.0 58.4 %shard_map.64 = bf16[128,1024]{1,0:T(8,128)(2,1)} custom-call(bf16[128,2048]{1,0:T(8,128)(2,1)} %query_ref.1, bf16[128,256]{1,0:T(8,128)(2,1)} %key_ref.1, bf16[128,256]{1,0:T(8,128)(2,1)} %value_ref.1, s32[4,128]{1,0:T(4,128)} %bitcast.1, f32[2,512,128]{2,1,0:T(8,128)} %constant.2.clone.table_ref, bf16[2048,1024]{1,0:T(8,128)(2,1)} %weight_ref.1), custom_call_target="tpu_custom_call" | custom-call | tf_op jit(solution)/shard_map/pallas_call | solution.py:410
  58.4 1.7 %copy.8 = bf16[128,1024]{1,0:T(8,128)(2,1)} copy(bf16[128,1024]{1,0:T(8,128)(2,1)} %shard_map.64) | data formatting | bytes 524288
where the time goes:
time: 60.3 us; the launch traced here: 60.1 us
  Pallas kernels  58.4 us (97%)
  local copies, waits for them, and re-layouts  1.67 us (3%)
    pallas_call x1, Pallas kernels, fused(): pl.pallas_call(functools.partial(fused_kernel, n, back), out_shape=jax.Sh...  58.4 us
    unnamed x1, local copies, waits for them, and re-layouts  1.67 us

commit v1 on v0

--- a/solution.py
+++ b/solution.py
@@ -105,12 +105,13 @@
 
 
 def fused_kernel(
-    n, back, query_ref, key_ref, value_ref, doc_ref, table_ref, weight_ref, out_ref,
-    query_in, key_in, table, docs, weight, rotated, bias, kv, gathered, total_lo, total_hi,
-    partial, quarters, summed, landed,
-    load_sem, weight_sem, kv_send, kv_recv, up_send, down_send, chunk_recv,
-    quarter_send, quarter_recv, result_send, result_recv, store_sem,
+    n, groups, back, query_ref, key_ref, value_ref, doc_ref, table_ref, weight_ref, out_ref,
+    query_in, key_in, table, docs, weight, lent, rotated, bias, kv, gathered, total_lo, total_hi,
+    partial, pair_in, crossing, cross_in, summed, landed, landed_aid,
+    load_sem, weight_sem, kv_send, kv_recv, up_send, down_send, chunk_recv, lend_send, lend_recv,
+    share_send, share_recv, pair_send, pair_recv, cross_send, cross_recv, result_send, result_recv, aid_recv, store_sem,
 ):
+    group = lax.axis_index("groups")
     ctx = lax.axis_index("ctx")
     tp = lax.axis_index("tp")
     rows = query_ref.shape[0]
@@ -122,6 +123,17 @@
     chunk_heads = chunk_width // HEAD_SIZE
     quarter = partial.shape[3]
     last = n - 1
+    lent_chunk = chunks - 1
+    pieces = lend_send.shape[0]
+    half_rows = chunk_width // groups
+    piece_rows = half_rows // pieces
+    is_edge = (ctx == 0) | (ctx == last)
+    is_helper = (ctx == 1) | (ctx == last - 1)
+    helped = jnp.where(ctx == 1, 0, last)
+    other_group = lax.rem(group + 1, groups)
+    pair = tp + 1 - 2 * lax.rem(tp, 2)
+    across = lax.rem(tp + 2, n)
+    pair_across = lax.rem(pair + 2, n)
 
     def remote(src, dst, send, recv, to_ctx, to_tp):
         return pltpu.make_async_remote_copy(
@@ -130,12 +142,32 @@
         )
 
     barrier = pltpu.get_barrier_semaphore()
-    for step in range(1, n * n):
-        pl.semaphore_signal(
-            barrier, inc=1,
-            device_id={"ctx": lax.rem(ctx + step // n, n), "tp": lax.rem(tp + step % n, n)},
-            device_id_type=MESH,
-        )
+
+    def greet(**device):
+        pl.semaphore_signal(barrier, inc=1, device_id=device, device_id_type=MESH)
+
+    @pl.when(ctx > 0)
+    def _():
+        greet(ctx=ctx - 1)
+
+    @pl.when(ctx < last)
+    def _():
+        greet(ctx=ctx + 1)
+
+    @pl.when(ctx == back)
+    def _():
+        greet(ctx=ctx - back)
+
+    for step in range(1, n):
+        greet(tp=lax.rem(tp + step, n))
+
+    @pl.when(is_helper)
+    def _():
+        greet(groups=other_group)
+
+    greetings = n - 1 + sum(
+        flag.astype(jnp.int32) for flag in (ctx > 0, ctx < last, ctx == 0, is_helper)
+    )
 
     first_row = pl.multiple_of(ctx * rows, rows)
     loads = [
@@ -154,7 +186,7 @@
         pltpu.make_async_copy(
             weight_ref.at[pl.ds(chunk * chunk_width, chunk_width)], weight.at[chunk], weight_sem.at[chunk]
         )
-        for chunk in range(chunks)
+        for chunk in [lent_chunk] + list(range(lent_chunk))
     ]
     for load in loads + value_loads + weight_loads:
         load.start()
@@ -175,7 +207,7 @@
         def _():
             kv[slot] = jnp.zeros(kv.shape[1:], kv.dtype)
 
-    pl.semaphore_wait(barrier, n * n - 1)
+    pl.semaphore_wait(barrier, greetings)
 
     def kv_copy(slot, head):
         return remote(
@@ -183,13 +215,19 @@
             lax.rem(ctx + 1, n), tp,
         )
 
-    def kv_sends(slot):
-        return (ctx < last) & (ctx >= back - slot)
-
-    @pl.when(ctx < last)
-    def _():
-        for head in range(kv_heads):
+    def kv_direct(head):
+        return remote(
+            kv.at[back, head], kv.at[0, head], kv_send.at[0, head], kv_recv.at[0, head], lax.rem(ctx + back, n), tp
+        )
+
+    for head in range(kv_heads):
+        @pl.when(ctx < last)
+        def _():
             kv_copy(back, head).start()
+
+        @pl.when(ctx == 0)
+        def _():
+            kv_direct(head).start()
 
     loads[2].wait()
     own_docs = jnp.broadcast_to(docs[pl.ds(ctx, 1), :], (rows, rows)).astype(jnp.float32).T
@@ -205,15 +243,35 @@
     for head in range(query_heads):
         rotated[head] = turn(query_in[:, head * HEAD_SIZE : (head + 1) * HEAD_SIZE])
 
-    for slot in range(back - 1, 0, -1):
-        for head in range(kv_heads):
-            @pl.when(ctx >= back - slot)
-            def _():
-                kv_copy(slot + 1, head).wait_recv()
-
-            @pl.when(kv_sends(slot))
-            def _():
-                kv_copy(slot, head).start()
+    weight_loads[0].wait()
+    forwards = (ctx >= back) & (ctx < last)
+
+    def take_kv(head):
+        kv_copy(back, head).wait_recv()
+
+        @pl.when(forwards)
+        def _():
+            kv_copy(back - 1, head).start()
+
+    for head in range(kv_heads):
+        @pl.when(ctx >= (1 if head == 0 else back))
+        def _():
+            take_kv(head)
+
+    def lend_copy(piece):
+        start = pl.multiple_of(group * half_rows + piece * piece_rows, piece_rows)
+        return remote(
+            weight.at[lent_chunk, pl.ds(start, piece_rows)], lent.at[pl.ds(start, piece_rows)],
+            lend_send.at[piece], lend_recv.at[piece], jnp.where(ctx == 0, 1, last - 1), tp,
+        )
+
+    def share_copy(piece, owner):
+        start = pl.multiple_of(owner * half_rows + piece * piece_rows, piece_rows)
+        here = lent.at[pl.ds(start, piece_rows)]
+        return pltpu.make_async_remote_copy(
+            src_ref=here, dst_ref=here, send_sem=share_send.at[piece], recv_sem=share_recv.at[piece],
+            device_id={"groups": other_group}, device_id_type=MESH,
+        )
 
     def up_copy(block, chunk):
         here = gathered.at[block, chunk]
@@ -222,12 +280,23 @@
     def down_copy(block, chunk):
         here = gathered.at[block, chunk]
         return remote(here, here, down_send.at[block, chunk], chunk_recv.at[block, chunk], lax.rem(ctx + last, n), tp)
+
+    def goes_up(chunk):
+        return ctx < (last - 1 if chunk == lent_chunk else last)
+
+    def goes_down(chunk):
+        return ctx > (1 if chunk == lent_chunk else 0)
 
     scale = HEAD_SIZE ** (-0.5) * math.log2(math.e)
     contract = (((1,), (1,)), ((), ()))
     for head in range(query_heads):
         kv_head = head // group_width
         if head % group_width == 0:
+            if kv_head > 0:
+                @pl.when((ctx >= 1) & (ctx < back))
+                def _():
+                    take_kv(kv_head)
+
             @pl.when(ctx >= back)
             def _():
                 kv_copy(1, kv_head).wait_recv()
@@ -247,36 +316,71 @@
         chunk, place = head // chunk_heads, head % chunk_heads
         gathered[ctx, chunk, :, place * HEAD_SIZE : (place + 1) * HEAD_SIZE] = (mixed / totals).astype(jnp.bfloat16)
         if place == chunk_heads - 1:
-            @pl.when(ctx < last)
+            @pl.when(goes_up(chunk))
             def _():
                 up_copy(ctx, chunk).start()
 
-            @pl.when(ctx > 0)
+            @pl.when(goes_down(chunk))
             def _():
                 down_copy(ctx, chunk).start()
 
-    def quarter_copy(block, hop):
-        to = lax.rem(tp + hop, n)
+    @pl.when(is_edge)
+    def _():
+        for piece in range(pieces):
+            lend_copy(piece).start()
+
+    def pair_copy(place, index):
         return remote(
-            partial.at[block, to], quarters.at[block, hop], quarter_send.at[block, hop], quarter_recv.at[block, hop],
-            ctx, to,
-        )
-
-    def project(block, chunk, total):
-        for hop in list(range(1, n)) + [0]:
-            part = lax.rem(tp + hop, n)
-            columns = pl.ds(pl.multiple_of(part * quarter, quarter), quarter)
+            partial.at[place, pair_across if index else pair], pair_in.at[place, index],
+            pair_send.at[place, index], pair_recv.at[place, index], ctx, pair,
+        )
+
+    def cross_copy(place):
+        return remote(
+            crossing.at[place], cross_in.at[place], cross_send.at[place], cross_recv.at[place], ctx, across
+        )
+
+    parts = (pair_across, pair, across, tp)
+
+    def part_columns(part):
+        return pl.ds(pl.multiple_of(part * quarter, quarter), quarter)
+
+    def emit(place, index, product):
+        partial[place, parts[index]] = product.astype(jnp.bfloat16)
+        if index < 2:
+            pair_copy(place, 1 - index).start()
+
+    def project(block, chunk, total, own):
+        for index, part in enumerate(parts):
             product = jnp.dot(
-                gathered[block, chunk], weight[chunk, :, columns], preferred_element_type=jnp.float32
+                gathered[block, chunk], weight[chunk, :, part_columns(part)], preferred_element_type=jnp.float32
             )
             if chunk > 0:
-                product = product + total[hop]
-            if chunk < chunks - 1:
-                total[hop] = product
+                product = product + total[index]
+            if chunk == lent_chunk:
+                emit(block, index, product)
+            elif chunk == lent_chunk - 1 and not own:
+                @pl.when(is_edge)
+                def _():
+                    emit(block, index, product)
+
+                @pl.when(jnp.logical_not(is_edge))
+                def _():
+                    total[index] = product
             else:
-                partial[block, part] = product.astype(jnp.bfloat16)
-                if hop:
-                    quarter_copy(block, hop).start()
+                total[index] = product
+
+    def cross(place):
+        pair_copy(place, 1).wait_recv()
+        value = partial[place, across].astype(jnp.float32) + pair_in[place, 1].astype(jnp.float32)
+        crossing[place] = value.astype(jnp.bfloat16)
+        cross_copy(place).start()
+
+    def collect(place):
+        pair_copy(place, 0).wait_recv()
+        value = partial[place, tp].astype(jnp.float32) + pair_in[place, 0].astype(jnp.float32)
+        cross_copy(place).wait_recv()
+        return (value + cross_in[place].astype(jnp.float32)).astype(jnp.bfloat16)
 
     def result_copy(block):
         return remote(
@@ -284,11 +388,7 @@
         )
 
     def finish(block):
-        value = partial[block, tp].astype(jnp.float32)
-        for hop in range(1, n):
-            quarter_copy(block, hop).wait_recv()
-            value = value + quarters[block, hop].astype(jnp.float32)
-        value = value.astype(jnp.bfloat16)
+        value = collect(block)
         mine = (block == ctx) & (tp == ctx)
 
         @pl.when(mine)
@@ -300,29 +400,75 @@
             summed[block] = value
             result_copy(block).start()
 
-    for load in weight_loads:
+    for load in weight_loads[1:]:
         load.wait()
     for chunk in range(chunks):
-        project(ctx, chunk, total_lo)
-
-    def finish_pair(step):
+        project(ctx, chunk, total_lo, True)
+
+    def both_sides(step, act):
         @pl.when(ctx - step >= 0)
         def _():
-            finish(lax.max(ctx - step, 0))
+            act(lax.max(ctx - step, 0))
 
         @pl.when((ctx + step <= last) & (step > 0))
         def _():
-            finish(lax.min(ctx + step, last))
+            act(lax.min(ctx + step, last))
+
+    def pass_on(piece):
+        lend_copy(piece).wait_recv()
+        share_copy(piece, group).start()
+
+    def aided(index):
+        return jnp.where(ctx == 1, ctx + index, ctx - index)
+
+    def aid_copy(index):
+        return remote(
+            summed.at[n + index], landed_aid.at[tp], result_send.at[n + index], aid_recv.at[tp],
+            aided(index), helped,
+        )
+
+    def aid():
+        for piece in range(pieces):
+            share_copy(piece, other_group).wait_recv()
+        for place in range(n - 1):
+            for index, part in enumerate(parts):
+                product = jnp.dot(
+                    gathered[aided(place), lent_chunk], lent[:, part_columns(part)],
+                    preferred_element_type=jnp.float32,
+                )
+                emit(n + place, index, product)
+            if place:
+                cross(n + place - 1)
+        cross(2 * n - 2)
+
+    def send_aid():
+        for index in range(n - 1):
+            value = collect(n + index)
+            if index == 0:
+                @pl.when(tp == helped)
+                def _():
+                    landed_aid[tp] = value
+
+                @pl.when(tp != helped)
+                def _():
+                    summed[n] = value
+                    aid_copy(0).start()
+            else:
+                summed[n + index] = value
+                aid_copy(index).start()
 
     def gather_step(step, carry):
         low, high = lax.max(ctx - step, 0), lax.min(ctx + step, last)
-        has_low, has_high = ctx - step >= 0, ctx + step <= last
         for chunk in range(chunks):
+            has_low, has_high = ctx - step >= 0, ctx + step <= last
+            if chunk == lent_chunk:
+                has_low, has_high = has_low & (ctx < last), has_high & (ctx > 0)
+
             @pl.when(has_low)
             def _():
                 up_copy(low, chunk).wait_recv()
 
-                @pl.when(ctx < last)
+                @pl.when(goes_up(chunk))
                 def _():
                     up_copy(low, chunk).start()
 
@@ -330,24 +476,43 @@
             def _():
                 down_copy(high, chunk).wait_recv()
 
-                @pl.when(ctx > 0)
+                @pl.when(goes_down(chunk))
                 def _():
                     down_copy(high, chunk).start()
 
             @pl.when(has_low)
             def _():
-                project(low, chunk, total_lo)
+                project(low, chunk, total_lo, False)
 
             @pl.when(has_high)
             def _():
-                project(high, chunk, total_hi)
-
-        finish_pair(step - 1)
+                project(high, chunk, total_hi, False)
+
+            @pl.when(is_helper & (step == 2))
+            def _():
+                pass_on(chunk)
+
+            if chunk == 0:
+                both_sides(step - 1, cross)
+
+        @pl.when(is_helper & (step == last))
+        def _():
+            aid()
+
+        both_sides(step - 1, finish)
         return carry
 
     lax.fori_loop(1, n, gather_step, 0)
-    finish_pair(last)
-
+    both_sides(last, cross)
+
+    @pl.when(is_helper)
+    def _():
+        send_aid()
+
+    both_sides(last, finish)
+
+    gets_aid = ((tp == 0) | (tp == last)) & (ctx != tp)
+    aid_here = is_helper & (tp == helped)
     for part in range(n):
         @pl.when(jnp.logical_not((tp == ctx) & (tp == part)))
         def _():
@@ -355,28 +520,56 @@
                 summed.at[0], landed.at[part], result_send.at[0], result_recv.at[part], ctx, part
             ).wait_recv()
 
+        @pl.when(gets_aid)
+        def _():
+            @pl.when(jnp.logical_not(aid_here & (tp == part)))
+            def _():
+                remote(
+                    summed.at[n], landed_aid.at[part], result_send.at[n], aid_recv.at[part], ctx, part
+                ).wait_recv()
+
+            whole = landed[part].astype(jnp.float32) + landed_aid[part].astype(jnp.float32)
+            landed[part] = whole.astype(jnp.bfloat16)
+
         pltpu.make_async_copy(
             landed.at[part], out_ref.at[:, pl.ds(part * quarter, quarter)], store_sem.at[part]
         ).start()
 
-    for slot in range(1, back + 1):
-        for head in range(kv_heads):
-            @pl.when(kv_sends(slot))
-            def _():
-                kv_copy(slot, head).wait_send()
+    for head in range(kv_heads):
+        @pl.when(ctx < last)
+        def _():
+            kv_copy(back, head).wait_send()
+
+        @pl.when(ctx == 0)
+        def _():
+            kv_direct(head).wait_send()
+
+        @pl.when(forwards)
+        def _():
+            kv_copy(back - 1, head).wait_send()
+
+    for piece in range(pieces):
+        @pl.when(is_edge)
+        def _():
+            lend_copy(piece).wait_send()
+
+        @pl.when(is_helper)
+        def _():
+            share_copy(piece, group).wait_send()
 
     def drain(block, carry):
         for chunk in range(chunks):
-            @pl.when((block <= ctx) & (ctx < last))
+            @pl.when((block <= ctx) & goes_up(chunk))
             def _():
                 up_copy(block, chunk).wait_send()
 
-            @pl.when((block >= ctx) & (ctx > 0))
+            @pl.when((block >= ctx) & goes_down(chunk))
             def _():
                 down_copy(block, chunk).wait_send()
 
-        for hop in range(1, n):
-            quarter_copy(block, hop).wait_send()
+        for index in range(2):
+            pair_copy(block, index).wait_send()
+        cross_copy(block).wait_send()
 
         @pl.when(jnp.logical_not((block == ctx) & (tp == ctx)))
         def _():
@@ -385,18 +578,36 @@
         return carry
 
     lax.fori_loop(0, n, drain, 0)
+
+    @pl.when(is_helper)
+    def _():
+        for index in range(n - 1):
+            for side in range(2):
+                pair_copy(n + index, side).wait_send()
+            cross_copy(n + index).wait_send()
+            if index == 0:
+                @pl.when(tp != helped)
+                def _():
+                    aid_copy(0).wait_send()
+            else:
+                aid_copy(index).wait_send()
+
     for part in range(n):
         pltpu.make_async_copy(
             landed.at[part], out_ref.at[:, pl.ds(part * quarter, quarter)], store_sem.at[part]
         ).wait()
 
 
-def fused(n, query_matrix, key_matrix, value_matrix, doc_ids, out_weight):
+def key_blocks_back(tokens, rows):
+    return -(-(tokens // 2 - 1) // rows)
+
+
+def fused(n, groups, query_matrix, key_matrix, value_matrix, doc_ids, out_weight):
     rows, query_width = query_matrix.shape
     query_heads, kv_heads = query_width // HEAD_SIZE, key_matrix.shape[1] // HEAD_SIZE
     features = out_weight.shape[1]
     tokens = doc_ids.shape[0]
-    back = -(-(tokens // 2 - 1) // rows)
+    back = key_blocks_back(tokens, rows)
     chunks = 4
     chunk_width = query_width // chunks
     quarter = features // n
@@ -408,7 +619,7 @@
     any_space = pl.BlockSpec(memory_space=pl.ANY)
     bf16, f32, dma = jnp.bfloat16, jnp.float32, pltpu.SemaphoreType.DMA
     return pl.pallas_call(
-        functools.partial(fused_kernel, n, back),
+        functools.partial(fused_kernel, n, groups, back),
         out_shape=jax.ShapeDtypeStruct((rows, features), bf16),
         in_specs=[any_space] * 6,
         out_specs=any_space,
@@ -418,14 +629,18 @@
             pltpu.VMEM((2, rows, HEAD_SIZE), f32),
             pltpu.VMEM((tokens // rows, rows), jnp.int32),
             pltpu.VMEM((chunks, chunk_width, features), bf16),
+            pltpu.VMEM((chunk_width, features), bf16),
             pltpu.VMEM((query_heads, rows, HEAD_SIZE), bf16),
             pltpu.VMEM((back + 1, rows, rows), f32),
             pltpu.VMEM((back + 1, kv_heads, 2, rows, HEAD_SIZE), bf16),
             pltpu.VMEM((n, chunks, rows, chunk_width), bf16),
             pltpu.VMEM((n, rows, quarter), f32),
             pltpu.VMEM((n, rows, quarter), f32),
-            pltpu.VMEM((n, n, rows, quarter), bf16),
-            pltpu.VMEM((n, n, rows, quarter), bf16),
+            pltpu.VMEM((2 * n - 1, n, rows, quarter), bf16),
+            pltpu.VMEM((2 * n - 1, 2, rows, quarter), bf16),
+            pltpu.VMEM((2 * n - 1, rows, quarter), bf16),
+            pltpu.VMEM((2 * n - 1, rows, quarter), bf16),
+            pltpu.VMEM((2 * n - 1, rows, quarter), bf16),
             pltpu.VMEM((n, rows, quarter), bf16),
             pltpu.VMEM((n, rows, quarter), bf16),
             dma((4 + kv_heads,)),
@@ -435,8 +650,15 @@
             dma((n, chunks)),
             dma((n, chunks)),
             dma((n, chunks)),
-            dma((n, n)),
-            dma((n, n)),
+            dma((chunks,)),
+            dma((chunks,)),
+            dma((chunks,)),
+            dma((chunks,)),
+            dma((2 * n - 1, 2)),
+            dma((2 * n - 1, 2)),
+            dma((2 * n - 1,)),
+            dma((2 * n - 1,)),
+            dma((2 * n - 1,)),
             dma((n,)),
             dma((n,)),
             dma((n,)),
@@ -454,8 +676,15 @@
         P("tp", "ctx"),
     )
     out_specs = P(("groups", "ctx"), "tp")
-    n = mesh.shape["ctx"]
-    body = functools.partial(fused, n) if n == mesh.shape["tp"] else on_device
+    n, groups = mesh.shape["ctx"], mesh.shape["groups"]
+
+    def body(*arrays):
+        query_matrix, doc_ids = arrays[0], arrays[3]
+        back = key_blocks_back(doc_ids.shape[0], query_matrix.shape[0])
+        if n == mesh.shape["tp"] and n == 4 and groups == 2 and back == 2:
+            return fused(n, groups, *arrays)
+        return on_device(*arrays)
+
     return jax.shard_map(
         body, mesh=mesh, in_specs=in_specs, out_specs=out_specs, check_vma=False
     )

time: 60.3 us -> 56.9 us (0.944)
  Pallas kernels: 58.4 us -> 55.1 us
    pallas_call x1, Pallas kernels: 58.4 us -> 55.1 us  [fused(): pl.pallas_call(functools.partial(fused_kernel, n, groups, back), out_shap...]
where the time goes in v1:
time: 56.9 us; the launch traced here: 56.8 us
  Pallas kernels  55.1 us (97%)
  local copies, waits for them, and re-layouts  1.67 us (3%)
    pallas_call x1, Pallas kernels, fused(): pl.pallas_call(functools.partial(fused_kernel, n, groups, back), out_shap...  55.1 us
    unnamed x1, local copies, waits for them, and re-layouts  1.67 us

profile of v1, /device:TPU:3, one launch (start us, length us, event | category | flops | bytes accessed | tf_op | source)
XLA Modules:
  0.0 56.8 jit_solution(10227509621033706341)
XLA Ops:
  0.0 55.1 %shard_map.64 = bf16[128,1024]{1,0:T(8,128)(2,1)} custom-call(bf16[128,2048]{1,0:T(8,128)(2,1)} %query_ref.1, bf16[128,256]{1,0:T(8,128)(2,1)} %key_ref.1, bf16[128,256]{1,0:T(8,128)(2,1)} %value_ref.1, s32[4,128]{1,0:T(4,128)} %bitcast.1, f32[2,512,128]{2,1,0:T(8,128)} %constant.2.clone.table_ref, bf16[2048,1024]{1,0:T(8,128)(2,1)} %weight_ref.1), custom_call_target="tpu_custom_call" | custom-call | tf_op jit(solution)/shard_map/pallas_call | solution.py:621
  55.1 1.7 %copy.8 = bf16[128,1024]{1,0:T(8,128)(2,1)} copy(bf16[128,1024]{1,0:T(8,128)(2,1)} %shard_map.64) | data formatting | bytes 524288

commit v2 on v1

--- a/solution.py
+++ b/solution.py
@@ -15,6 +15,8 @@
 
 
 rope_base = 1000000.0
+
+LENT_SHARE = 3 / 16
 
 
 def rotary_tables(rows, token_positions, heads):
@@ -106,10 +108,11 @@
 
 def fused_kernel(
     n, groups, back, query_ref, key_ref, value_ref, doc_ref, table_ref, weight_ref, out_ref,
-    query_in, key_in, table, docs, weight, lent, rotated, bias, kv, gathered, total_lo, total_hi,
-    partial, pair_in, crossing, cross_in, summed, landed, landed_aid,
-    load_sem, weight_sem, kv_send, kv_recv, up_send, down_send, chunk_recv, lend_send, lend_recv,
-    share_send, share_recv, pair_send, pair_recv, cross_send, cross_recv, result_send, result_recv, aid_recv, store_sem,
+    query_in, key_in, table, docs, weight, lent, rotated, bias, kv, gathered, sums,
+    partial, pair_in, crossing, cross_in, summed, landed, halves, landed_far, landed_aid,
+    load_sem, weight_sem, kv_send, kv_recv, away_send, edge_send, chunk_recv, lend_send, lend_recv,
+    share_send, share_recv, pair_send, pair_recv, cross_send, cross_recv, result_send, result_recv,
+    half_send, far_recv, aid_recv, store_sem,
 ):
     group = lax.axis_index("groups")
     ctx = lax.axis_index("ctx")
@@ -118,15 +121,19 @@
     kv_heads = key_ref.shape[1] // HEAD_SIZE
     query_heads = query_ref.shape[1] // HEAD_SIZE
     group_width = query_heads // kv_heads
-    chunks = gathered.shape[1]
-    chunk_width = gathered.shape[3]
-    chunk_heads = chunk_width // HEAD_SIZE
+    ends = chunk_ends(query_heads, groups)
+    starts = [0] + ends[:-1]
+    chunks = len(ends)
     quarter = partial.shape[3]
     last = n - 1
     lent_chunk = chunks - 1
     pieces = lend_send.shape[0]
-    half_rows = chunk_width // groups
+    half_rows = lent.shape[0] // groups
     piece_rows = half_rows // pieces
+
+    def columns_of(chunk):
+        return pl.ds(starts[chunk] * HEAD_SIZE, (ends[chunk] - starts[chunk]) * HEAD_SIZE)
+
     is_edge = (ctx == 0) | (ctx == last)
     is_helper = (ctx == 1) | (ctx == last - 1)
     helped = jnp.where(ctx == 1, 0, last)
@@ -184,7 +191,7 @@
     ]
     weight_loads = [
         pltpu.make_async_copy(
-            weight_ref.at[pl.ds(chunk * chunk_width, chunk_width)], weight.at[chunk], weight_sem.at[chunk]
+            weight_ref.at[columns_of(chunk)], weight.at[columns_of(chunk)], weight_sem.at[chunk]
         )
         for chunk in [lent_chunk] + list(range(lent_chunk))
     ]
@@ -228,6 +235,28 @@
         @pl.when(ctx == 0)
         def _():
             kv_direct(head).start()
+
+    def lend_copy(piece):
+        start = pl.multiple_of(group * half_rows + piece * piece_rows, piece_rows)
+        return remote(
+            weight.at[pl.ds(starts[lent_chunk] * HEAD_SIZE + start, piece_rows)], lent.at[pl.ds(start, piece_rows)],
+            lend_send.at[piece], lend_recv.at[piece], jnp.where(ctx == 0, 1, last - 1), tp,
+        )
+
+    def share_copy(piece, owner):
+        start = pl.multiple_of(owner * half_rows + piece * piece_rows, piece_rows)
+        here = lent.at[pl.ds(start, piece_rows)]
+        return pltpu.make_async_remote_copy(
+            src_ref=here, dst_ref=here, send_sem=share_send.at[piece], recv_sem=share_recv.at[piece],
+            device_id={"groups": other_group}, device_id_type=MESH,
+        )
+
+    weight_loads[0].wait()
+
+    @pl.when(is_edge)
+    def _():
+        for piece in range(pieces):
+            lend_copy(piece).start()
 
     loads[2].wait()
     own_docs = jnp.broadcast_to(docs[pl.ds(ctx, 1), :], (rows, rows)).astype(jnp.float32).T
@@ -243,7 +272,7 @@
     for head in range(query_heads):
         rotated[head] = turn(query_in[:, head * HEAD_SIZE : (head + 1) * HEAD_SIZE])
 
-    weight_loads[0].wait()
+
     forwards = (ctx >= back) & (ctx < last)
 
     def take_kv(head):
@@ -258,45 +287,32 @@
         def _():
             take_kv(head)
 
-    def lend_copy(piece):
-        start = pl.multiple_of(group * half_rows + piece * piece_rows, piece_rows)
-        return remote(
-            weight.at[lent_chunk, pl.ds(start, piece_rows)], lent.at[pl.ds(start, piece_rows)],
-            lend_send.at[piece], lend_recv.at[piece], jnp.where(ctx == 0, 1, last - 1), tp,
-        )
-
-    def share_copy(piece, owner):
-        start = pl.multiple_of(owner * half_rows + piece * piece_rows, piece_rows)
-        here = lent.at[pl.ds(start, piece_rows)]
-        return pltpu.make_async_remote_copy(
-            src_ref=here, dst_ref=here, send_sem=share_send.at[piece], recv_sem=share_recv.at[piece],
-            device_id={"groups": other_group}, device_id_type=MESH,
-        )
-
-    def up_copy(block, chunk):
-        here = gathered.at[block, chunk]
-        return remote(here, here, up_send.at[block, chunk], chunk_recv.at[block, chunk], lax.rem(ctx + 1, n), tp)
-
-    def down_copy(block, chunk):
-        here = gathered.at[block, chunk]
-        return remote(here, here, down_send.at[block, chunk], chunk_recv.at[block, chunk], lax.rem(ctx + last, n), tp)
-
-    def goes_up(chunk):
-        return ctx < (last - 1 if chunk == lent_chunk else last)
-
-    def goes_down(chunk):
-        return ctx > (1 if chunk == lent_chunk else 0)
+    away = jnp.where(ctx < n // 2, 1, -1)
+
+    def block_at(distance):
+        return ctx + distance * away
+
+    def chunk_copy(block, chunk, send, to_ctx):
+        here = gathered.at[block, :, columns_of(chunk)]
+        return remote(here, here, send.at[block, chunk], chunk_recv.at[block, chunk], to_ctx, tp)
+
+    def away_copy(block, chunk):
+        return chunk_copy(block, chunk, away_send, ctx + away)
+
+    def edge_copy(block, chunk):
+        return chunk_copy(block, chunk, edge_send, helped)
 
     scale = HEAD_SIZE ** (-0.5) * math.log2(math.e)
     contract = (((1,), (1,)), ((), ()))
     for head in range(query_heads):
         kv_head = head // group_width
+        if head == ends[0]:
+            @pl.when((ctx >= 1) & (ctx < back))
+            def _():
+                for other in range(1, kv_heads):
+                    take_kv(other)
+
         if head % group_width == 0:
-            if kv_head > 0:
-                @pl.when((ctx >= 1) & (ctx < back))
-                def _():
-                    take_kv(kv_head)
-
             @pl.when(ctx >= back)
             def _():
                 kv_copy(1, kv_head).wait_recv()
@@ -313,21 +329,23 @@
             jnp.dot(weights[slot].astype(jnp.bfloat16), kv[slot, kv_head, 1], preferred_element_type=jnp.float32)
             for slot in range(back + 1)
         )
-        chunk, place = head // chunk_heads, head % chunk_heads
-        gathered[ctx, chunk, :, place * HEAD_SIZE : (place + 1) * HEAD_SIZE] = (mixed / totals).astype(jnp.bfloat16)
-        if place == chunk_heads - 1:
-            @pl.when(goes_up(chunk))
-            def _():
-                up_copy(ctx, chunk).start()
-
-            @pl.when(goes_down(chunk))
-            def _():
-                down_copy(ctx, chunk).start()
-
-    @pl.when(is_edge)
-    def _():
-        for piece in range(pieces):
-            lend_copy(piece).start()
+        gathered[ctx, :, head * HEAD_SIZE : (head + 1) * HEAD_SIZE] = (mixed / totals).astype(jnp.bfloat16)
+        if head + 1 in ends:
+            chunk = ends.index(head + 1)
+            away_copy(ctx, chunk).start()
+            if chunk != lent_chunk:
+                @pl.when(is_helper)
+                def _():
+                    edge_copy(ctx, chunk).start()
+
+    def pass_on(piece):
+        lend_copy(piece).wait_recv()
+        share_copy(piece, group).start()
+
+    @pl.when(is_helper)
+    def _():
+        pass_on(0)
+        pass_on(1)
 
     def pair_copy(place, index):
         return remote(
@@ -350,13 +368,14 @@
         if index < 2:
             pair_copy(place, 1 - index).start()
 
-    def project(block, chunk, total, own):
+    def project(block, chunk, keep, own):
         for index, part in enumerate(parts):
             product = jnp.dot(
-                gathered[block, chunk], weight[chunk, :, part_columns(part)], preferred_element_type=jnp.float32
+                gathered[block, :, columns_of(chunk)], weight[columns_of(chunk), part_columns(part)],
+                preferred_element_type=jnp.float32,
             )
             if chunk > 0:
-                product = product + total[index]
+                product = product + sums[keep, index]
             if chunk == lent_chunk:
                 emit(block, index, product)
             elif chunk == lent_chunk - 1 and not own:
@@ -366,9 +385,9 @@
 
                 @pl.when(jnp.logical_not(is_edge))
                 def _():
-                    total[index] = product
+                    sums[keep, index] = product
             else:
-                total[index] = product
+                sums[keep, index] = product
 
     def cross(place):
         pair_copy(place, 1).wait_recv()
@@ -403,131 +422,153 @@
     for load in weight_loads[1:]:
         load.wait()
     for chunk in range(chunks):
-        project(ctx, chunk, total_lo, True)
-
-    def both_sides(step, act):
-        @pl.when(ctx - step >= 0)
-        def _():
-            act(lax.max(ctx - step, 0))
-
-        @pl.when((ctx + step <= last) & (step > 0))
-        def _():
-            act(lax.min(ctx + step, last))
-
-    def pass_on(piece):
-        lend_copy(piece).wait_recv()
-        share_copy(piece, group).start()
-
-    def aided(index):
-        return jnp.where(ctx == 1, ctx + index, ctx - index)
+        project(ctx, chunk, 0, True)
 
     def aid_copy(index):
         return remote(
             summed.at[n + index], landed_aid.at[tp], result_send.at[n + index], aid_recv.at[tp],
-            aided(index), helped,
-        )
-
-    def aid():
+            block_at(index), helped,
+        )
+
+    def far_copy():
+        return remote(
+            halves, landed_far.at[tp], half_send, far_recv.at[tp], last - ctx, ctx
+        )
+
+    def pair_sum(place, index):
+        pair_copy(place, index).wait_recv()
+        part = across if index else tp
+        value = partial[place, part].astype(jnp.float32) + pair_in[place, index].astype(jnp.float32)
+        return value.astype(jnp.bfloat16)
+
+    def finish_far(place):
+        for index in (1, 0):
+            halves[index] = pair_sum(place, index)
+        far_copy().start()
+
+    def aid(index):
+        for position, part in enumerate(parts):
+            product = jnp.dot(
+                gathered[block_at(index), :, columns_of(lent_chunk)], lent[:, part_columns(part)],
+                preferred_element_type=jnp.float32,
+            )
+            emit(n + index, position, product)
+
+    def finish_aid(index):
+        value = collect(n + index)
+        if index == 0:
+            @pl.when(tp == helped)
+            def _():
+                landed_aid[tp] = value
+
+            @pl.when(tp != helped)
+            def _():
+                summed[n] = value
+                aid_copy(0).start()
+        else:
+            summed[n + index] = value
+            aid_copy(index).start()
+
+    def take(block, chunk, forward):
+        away_copy(block, chunk).wait_recv()
+        if forward is not None:
+            forward(block, chunk).start()
+
+    @pl.when(is_edge)
+    def _():
+        def gather_step(distance, carry):
+            block = block_at(distance)
+            for chunk in range(lent_chunk):
+                take(block, chunk, None)
+                project(block, chunk, 1, False)
+                if chunk == 0:
+                    cross(block_at(distance - 1))
+                if chunk == 1:
+                    finish(block_at(distance - 1))
+            return carry
+
+        lax.fori_loop(1, n, gather_step, 0)
+        finish_far(last - ctx)
+
+    @pl.when(is_helper)
+    def _():
+        def near(chunk):
+            take(helped, chunk, away_copy)
+            project(helped, chunk, 0, False)
+
+        def far(distance, chunk):
+            take(block_at(distance), chunk, edge_copy if chunk < lent_chunk else None)
+            project(block_at(distance), chunk, distance, False)
+
+        pass_on(2)
+        far(1, 0)
+        pass_on(3)
+        far(1, 1)
+        cross(ctx)
+        near(0)
+        far(1, 2)
+        far(1, lent_chunk)
+        near(1)
+        finish(ctx)
+        near(2)
+        cross(block_at(1))
+        far(2, 0)
         for piece in range(pieces):
             share_copy(piece, other_group).wait_recv()
-        for place in range(n - 1):
-            for index, part in enumerate(parts):
-                product = jnp.dot(
-                    gathered[aided(place), lent_chunk], lent[:, part_columns(part)],
-                    preferred_element_type=jnp.float32,
-                )
-                emit(n + place, index, product)
-            if place:
-                cross(n + place - 1)
-        cross(2 * n - 2)
-
-    def send_aid():
-        for index in range(n - 1):
-            value = collect(n + index)
-            if index == 0:
-                @pl.when(tp == helped)
-                def _():
-                    landed_aid[tp] = value
-
-                @pl.when(tp != helped)
-                def _():
-                    summed[n] = value
-                    aid_copy(0).start()
-            else:
-                summed[n + index] = value
-                aid_copy(index).start()
-
-    def gather_step(step, carry):
-        low, high = lax.max(ctx - step, 0), lax.min(ctx + step, last)
-        for chunk in range(chunks):
-            has_low, has_high = ctx - step >= 0, ctx + step <= last
-            if chunk == lent_chunk:
-                has_low, has_high = has_low & (ctx < last), has_high & (ctx > 0)
-
-            @pl.when(has_low)
-            def _():
-                up_copy(low, chunk).wait_recv()
-
-                @pl.when(goes_up(chunk))
-                def _():
-                    up_copy(low, chunk).start()
-
-            @pl.when(has_high)
-            def _():
-                down_copy(high, chunk).wait_recv()
-
-                @pl.when(goes_down(chunk))
-                def _():
-                    down_copy(high, chunk).start()
-
-            @pl.when(has_low)
-            def _():
-                project(low, chunk, total_lo, False)
-
-            @pl.when(has_high)
-            def _():
-                project(high, chunk, total_hi, False)
-
-            @pl.when(is_helper & (step == 2))
-            def _():
-                pass_on(chunk)
-
-            if chunk == 0:
-                both_sides(step - 1, cross)
-
-        @pl.when(is_helper & (step == last))
-        def _():
-            aid()
-
-        both_sides(step - 1, finish)
-        return carry
-
-    lax.fori_loop(1, n, gather_step, 0)
-    both_sides(last, cross)
-
-    @pl.when(is_helper)
-    def _():
-        send_aid()
-
-    both_sides(last, finish)
-
+        aid(1)
+        aid(0)
+        far(2, 1)
+        cross(n + 1)
+        cross(n)
+        finish(block_at(1))
+        near(lent_chunk)
+        far(2, 2)
+        cross(helped)
+        far(2, lent_chunk)
+        aid(2)
+        cross(block_at(2))
+        cross(n + 2)
+        finish_aid(1)
+        finish_aid(0)
+        finish(helped)
+        finish(block_at(2))
+        finish_aid(2)
+
+    is_far = is_edge & (tp == last - ctx)
     gets_aid = ((tp == 0) | (tp == last)) & (ctx != tp)
     aid_here = is_helper & (tp == helped)
+
+    @pl.when(is_far)
+    def _():
+        for part in range(n):
+            far = far_recv.at[part]
+            remote(halves, landed_far.at[part], half_send, far, ctx, part).wait_recv()
+
+    @pl.when(gets_aid)
+    def _():
+        for part in range(n):
+            @pl.when(jnp.logical_not(aid_here & (tp == part)))
+            def _():
+                here = aid_recv.at[part]
+                remote(summed.at[n], landed_aid.at[part], result_send.at[n], here, ctx, part).wait_recv()
+
+    def both_halves(landing, part):
+        return landing[part, 0].astype(jnp.float32) + landing[(part + 2) % n, 1].astype(jnp.float32)
+
     for part in range(n):
-        @pl.when(jnp.logical_not((tp == ctx) & (tp == part)))
+        @pl.when(jnp.logical_not(is_far | ((tp == ctx) & (tp == part))))
         def _():
             remote(
                 summed.at[0], landed.at[part], result_send.at[0], result_recv.at[part], ctx, part
             ).wait_recv()
 
-        @pl.when(gets_aid)
-        def _():
-            @pl.when(jnp.logical_not(aid_here & (tp == part)))
-            def _():
-                remote(
-                    summed.at[n], landed_aid.at[part], result_send.at[n], aid_recv.at[part], ctx, part
-                ).wait_recv()
-
+        @pl.when(is_far)
+        def _():
+            whole = both_halves(landed_far, part) + landed_aid[part].astype(jnp.float32)
+            landed[part] = whole.astype(jnp.bfloat16)
+
+        @pl.when(gets_aid & jnp.logical_not(is_far))
+        def _():
             whole = landed[part].astype(jnp.float32) + landed_aid[part].astype(jnp.float32)
             landed[part] = whole.astype(jnp.bfloat16)
 
@@ -559,25 +600,35 @@
 
     def drain(block, carry):
         for chunk in range(chunks):
-            @pl.when((block <= ctx) & goes_up(chunk))
+            @pl.when((block == ctx) | (is_helper & (block == helped)))
             def _():
-                up_copy(block, chunk).wait_send()
-
-            @pl.when((block >= ctx) & goes_down(chunk))
-            def _():
-                down_copy(block, chunk).wait_send()
+                away_copy(block, chunk).wait_send()
+
+            if chunk < lent_chunk:
+                @pl.when(is_helper & (block != helped))
+                def _():
+                    edge_copy(block, chunk).wait_send()
 
         for index in range(2):
             pair_copy(block, index).wait_send()
-        cross_copy(block).wait_send()
-
-        @pl.when(jnp.logical_not((block == ctx) & (tp == ctx)))
+
+        far_block = is_edge & (block == last - ctx)
+
+        @pl.when(jnp.logical_not(far_block))
+        def _():
+            cross_copy(block).wait_send()
+
+        @pl.when(jnp.logical_not(far_block | ((block == ctx) & (tp == ctx))))
         def _():
             result_copy(block).wait_send()
 
         return carry
 
     lax.fori_loop(0, n, drain, 0)
+
+    @pl.when(is_edge)
+    def _():
+        far_copy().wait_send()
 
     @pl.when(is_helper)
     def _():
@@ -598,6 +649,12 @@
         ).wait()
 
 
+def chunk_ends(heads, groups):
+    lent = max(1, round(heads * LENT_SHARE))
+    kept = heads - lent
+    return [heads // 4, heads // 2, kept, heads]
+
+
 def key_blocks_back(tokens, rows):
     return -(-(tokens // 2 - 1) // rows)
 
@@ -608,8 +665,9 @@
     features = out_weight.shape[1]
     tokens = doc_ids.shape[0]
     back = key_blocks_back(tokens, rows)
-    chunks = 4
-    chunk_width = query_width // chunks
+    chunks = len(chunk_ends(query_heads, groups))
+    lent_rows = query_width - chunk_ends(query_heads, groups)[-2] * HEAD_SIZE
+    pieces = 4
     quarter = features // n
     half = HEAD_SIZE // 2
     frequency = np.power(np.float32(rope_base), -np.arange(half, dtype=np.float32) * np.float32(2.0 / HEAD_SIZE))
@@ -628,20 +686,21 @@
             pltpu.VMEM((rows, kv_heads * HEAD_SIZE), bf16),
             pltpu.VMEM((2, rows, HEAD_SIZE), f32),
             pltpu.VMEM((tokens // rows, rows), jnp.int32),
-            pltpu.VMEM((chunks, chunk_width, features), bf16),
-            pltpu.VMEM((chunk_width, features), bf16),
+            pltpu.VMEM((query_width, features), bf16),
+            pltpu.VMEM((lent_rows, features), bf16),
             pltpu.VMEM((query_heads, rows, HEAD_SIZE), bf16),
             pltpu.VMEM((back + 1, rows, rows), f32),
             pltpu.VMEM((back + 1, kv_heads, 2, rows, HEAD_SIZE), bf16),
-            pltpu.VMEM((n, chunks, rows, chunk_width), bf16),
-            pltpu.VMEM((n, rows, quarter), f32),
-            pltpu.VMEM((n, rows, quarter), f32),
+            pltpu.VMEM((n, rows, query_width), bf16),
+            pltpu.VMEM((3, n, rows, quarter), f32),
             pltpu.VMEM((2 * n - 1, n, rows, quarter), bf16),
             pltpu.VMEM((2 * n - 1, 2, rows, quarter), bf16),
             pltpu.VMEM((2 * n - 1, rows, quarter), bf16),
             pltpu.VMEM((2 * n - 1, rows, quarter), bf16),
             pltpu.VMEM((2 * n - 1, rows, quarter), bf16),
             pltpu.VMEM((n, rows, quarter), bf16),
+            pltpu.VMEM((2, rows, quarter), bf16),
+            pltpu.VMEM((n, 2, rows, quarter), bf16),
             pltpu.VMEM((n, rows, quarter), bf16),
             dma((4 + kv_heads,)),
             dma((chunks,)),
@@ -650,15 +709,17 @@
             dma((n, chunks)),
             dma((n, chunks)),
             dma((n, chunks)),
-            dma((chunks,)),
-            dma((chunks,)),
-            dma((chunks,)),
-            dma((chunks,)),
+            dma((pieces,)),
+            dma((pieces,)),
+            dma((pieces,)),
+            dma((pieces,)),
             dma((2 * n - 1, 2)),
             dma((2 * n - 1, 2)),
             dma((2 * n - 1,)),
             dma((2 * n - 1,)),
             dma((2 * n - 1,)),
+            dma((n,)),
+            dma,
             dma((n,)),
             dma((n,)),
             dma((n,)),

time: 56.9 us -> 53.6 us (0.942)
  Pallas kernels: 55.1 us -> 51.7 us
    pallas_call x1, Pallas kernels: 55.1 us -> 51.7 us  [fused(): pl.pallas_call(functools.partial(fused_kernel, n, groups, back), out_shap...]
where the time goes in v2:
time: 53.6 us; the launch traced here: 53.4 us
  Pallas kernels  51.7 us (96%)
  local copies, waits for them, and re-layouts  1.67 us (3%)
    pallas_call x1, Pallas kernels, fused(): pl.pallas_call(functools.partial(fused_kernel, n, groups, back), out_shap...  51.7 us
    unnamed x1, local copies, waits for them, and re-layouts  1.67 us

profile of v2, /device:TPU:3, one launch (start us, length us, event | category | flops | bytes accessed | tf_op | source)
XLA Modules:
  0.0 53.4 jit_solution(17299478450977887270)
XLA Ops:
  0.0 51.7 %shard_map.64 = bf16[128,1024]{1,0:T(8,128)(2,1)} custom-call(bf16[128,2048]{1,0:T(8,128)(2,1)} %query_ref.1, bf16[128,256]{1,0:T(8,128)(2,1)} %key_ref.1, bf16[128,256]{1,0:T(8,128)(2,1)} %value_ref.1, s32[4,128]{1,0:T(4,128)} %bitcast.1, f32[2,512,128]{2,1,0:T(8,128)} %constant.2.clone.table_ref, bf16[2048,1024]{1,0:T(8,128)(2,1)} %weight_ref.1), custom_call_target="tpu_custom_call" | custom-call | tf_op jit(solution)/shard_map/pallas_call | solution.py:679
  51.8 1.7 %copy.8 = bf16[128,1024]{1,0:T(8,128)(2,1)} copy(bf16[128,1024]{1,0:T(8,128)(2,1)} %shard_map.64) | data formatting | bytes 524288

commit v3 on v2

--- a/solution.py
+++ b/solution.py
@@ -112,7 +112,7 @@
     partial, pair_in, crossing, cross_in, summed, landed, halves, landed_far, landed_aid,
     load_sem, weight_sem, kv_send, kv_recv, away_send, edge_send, chunk_recv, lend_send, lend_recv,
     share_send, share_recv, pair_send, pair_recv, cross_send, cross_recv, result_send, result_recv,
-    half_send, far_recv, aid_recv, store_sem,
+    half_send, far_recv, aid_recv,
 ):
     group = lax.axis_index("groups")
     ctx = lax.axis_index("ctx")
@@ -232,9 +232,10 @@
         def _():
             kv_copy(back, head).start()
 
-        @pl.when(ctx == 0)
-        def _():
-            kv_direct(head).start()
+        if head == 0:
+            @pl.when(ctx == 0)
+            def _():
+                kv_direct(head).start()
 
     def lend_copy(piece):
         start = pl.multiple_of(group * half_rows + piece * piece_rows, piece_rows)
@@ -273,12 +274,13 @@
         rotated[head] = turn(query_in[:, head * HEAD_SIZE : (head + 1) * HEAD_SIZE])
 
 
-    forwards = (ctx >= back) & (ctx < last)
+    def forwards(head):
+        return (ctx >= (back if head == 0 else back - 1)) & (ctx < last)
 
     def take_kv(head):
         kv_copy(back, head).wait_recv()
 
-        @pl.when(forwards)
+        @pl.when(forwards(head))
         def _():
             kv_copy(back - 1, head).start()
 
@@ -306,7 +308,7 @@
     contract = (((1,), (1,)), ((), ()))
     for head in range(query_heads):
         kv_head = head // group_width
-        if head == ends[0]:
+        if head == ends[1] - 1:
             @pl.when((ctx >= 1) & (ctx < back))
             def _():
                 for other in range(1, kv_heads):
@@ -430,9 +432,12 @@
             block_at(index), helped,
         )
 
+    far_block = jnp.where(ctx < n // 2, last, 0)
+    sends_far = ctx != 1
+
     def far_copy():
         return remote(
-            halves, landed_far.at[tp], half_send, far_recv.at[tp], last - ctx, ctx
+            halves, landed_far.at[tp], half_send, far_recv.at[tp], far_block, ctx
         )
 
     def pair_sum(place, index):
@@ -441,9 +446,9 @@
         value = partial[place, part].astype(jnp.float32) + pair_in[place, index].astype(jnp.float32)
         return value.astype(jnp.bfloat16)
 
-    def finish_far(place):
+    def finish_far():
         for index in (1, 0):
-            halves[index] = pair_sum(place, index)
+            halves[index] = pair_sum(far_block, index)
         far_copy().start()
 
     def aid(index):
@@ -479,62 +484,104 @@
         def gather_step(distance, carry):
             block = block_at(distance)
             for chunk in range(lent_chunk):
+                if chunk == lent_chunk - 1:
+                    finish(block_at(distance - 1))
                 take(block, chunk, None)
                 project(block, chunk, 1, False)
                 if chunk == 0:
                     cross(block_at(distance - 1))
-                if chunk == 1:
-                    finish(block_at(distance - 1))
             return carry
 
         lax.fori_loop(1, n, gather_step, 0)
-        finish_far(last - ctx)
-
-    @pl.when(is_helper)
-    def _():
-        def near(chunk):
-            take(helped, chunk, away_copy)
-            project(helped, chunk, 0, False)
-
-        def far(distance, chunk):
-            take(block_at(distance), chunk, edge_copy if chunk < lent_chunk else None)
-            project(block_at(distance), chunk, distance, False)
-
-        pass_on(2)
-        far(1, 0)
-        pass_on(3)
-        far(1, 1)
-        cross(ctx)
-        near(0)
-        far(1, 2)
-        far(1, lent_chunk)
-        near(1)
-        finish(ctx)
-        near(2)
-        cross(block_at(1))
-        far(2, 0)
+        finish_far()
+
+    def near(chunk):
+        take(helped, chunk, away_copy)
+        project(helped, chunk, 0, False)
+
+    def far(distance, chunk):
+        take(block_at(distance), chunk, edge_copy if chunk < lent_chunk else None)
+        project(block_at(distance), chunk, distance, False)
+
+    def aid_both():
         for piece in range(pieces):
             share_copy(piece, other_group).wait_recv()
         aid(1)
         aid(0)
+
+    def last_chunks():
+        far(2, lent_chunk)
+        aid(2)
+        cross(n + 2)
+
+    @pl.when(ctx == 1)
+    def _():
+        far(1, 0)
+        pass_on(2)
+        far(1, 1)
+        pass_on(3)
+        cross(ctx)
+        near(0)
+        far(1, 2)
+        far(1, 3)
+        near(1)
+        finish(ctx)
+        far(1, lent_chunk)
+        near(2)
+        cross(block_at(1))
+        far(2, 0)
+        aid_both()
+        near(3)
         far(2, 1)
         cross(n + 1)
         cross(n)
-        finish(block_at(1))
         near(lent_chunk)
         far(2, 2)
+        finish(block_at(1))
         cross(helped)
-        far(2, lent_chunk)
-        aid(2)
-        cross(block_at(2))
-        cross(n + 2)
+        far(2, 3)
         finish_aid(1)
+        last_chunks()
+        cross(far_block)
         finish_aid(0)
         finish(helped)
-        finish(block_at(2))
         finish_aid(2)
-
-    is_far = is_edge & (tp == last - ctx)
+        finish(far_block)
+
+    @pl.when(ctx == last - 1)
+    def _():
+        pass_on(2)
+        far(1, 0)
+        pass_on(3)
+        near(0)
+        far(1, 1)
+        cross(ctx)
+        near(1)
+        far(1, 2)
+        far(1, 3)
+        near(2)
+        far(1, lent_chunk)
+        finish(ctx)
+        near(3)
+        cross(block_at(1))
+        near(lent_chunk)
+        aid_both()
+        far(2, 0)
+        cross(helped)
+        cross(n + 1)
+        cross(n)
+        far(2, 1)
+        far(2, 2)
+        finish(block_at(1))
+        finish(helped)
+        far(2, 3)
+        finish_aid(1)
+        last_chunks()
+        finish_far()
+        finish_aid(0)
+        finish_aid(2)
+
+    is_far = ((ctx == 0) & (tp >= n // 2)) | ((ctx == last) & (tp == 0))
     gets_aid = ((tp == 0) | (tp == last)) & (ctx != tp)
     aid_here = is_helper & (tp == helped)
 
@@ -562,30 +609,37 @@
                 summed.at[0], landed.at[part], result_send.at[0], result_recv.at[part], ctx, part
             ).wait_recv()
 
-        @pl.when(is_far)
+        columns = pl.ds(part * quarter, quarter)
+
+        @pl.when(is_far & jnp.logical_not(gets_aid))
+        def _():
+            out_ref[:, columns] = both_halves(landed_far, part).astype(jnp.bfloat16)
+
+        @pl.when(is_far & gets_aid)
         def _():
             whole = both_halves(landed_far, part) + landed_aid[part].astype(jnp.float32)
-            landed[part] = whole.astype(jnp.bfloat16)
+            out_ref[:, columns] = whole.astype(jnp.bfloat16)
 
         @pl.when(gets_aid & jnp.logical_not(is_far))
         def _():
             whole = landed[part].astype(jnp.float32) + landed_aid[part].astype(jnp.float32)
-            landed[part] = whole.astype(jnp.bfloat16)
-
-        pltpu.make_async_copy(
-            landed.at[part], out_ref.at[:, pl.ds(part * quarter, quarter)], store_sem.at[part]
-        ).start()
+            out_ref[:, columns] = whole.astype(jnp.bfloat16)
+
+        @pl.when(jnp.logical_not(gets_aid | is_far))
+        def _():
+            out_ref[:, columns] = landed[part]
 
     for head in range(kv_heads):
         @pl.when(ctx < last)
         def _():
             kv_copy(back, head).wait_send()
 
-        @pl.when(ctx == 0)
-        def _():
-            kv_direct(head).wait_send()
-
-        @pl.when(forwards)
+        if head == 0:
+            @pl.when(ctx == 0)
+            def _():
+                kv_direct(head).wait_send()
+
+        @pl.when(forwards(head))
         def _():
             kv_copy(back - 1, head).wait_send()
 
@@ -612,13 +666,13 @@
         for index in range(2):
             pair_copy(block, index).wait_send()
 
-        far_block = is_edge & (block == last - ctx)
-
-        @pl.when(jnp.logical_not(far_block))
+        @pl.when((block != far_block) | jnp.logical_not(sends_far))
         def _():
             cross_copy(block).wait_send()
 
-        @pl.when(jnp.logical_not(far_block | ((block == ctx) & (tp == ctx))))
+        own_part = (block == ctx) & (tp == ctx)
+
+        @pl.when(((block != far_block) | jnp.logical_not(sends_far)) & jnp.logical_not(own_part))
         def _():
             result_copy(block).wait_send()
 
@@ -626,7 +680,7 @@
 
     lax.fori_loop(0, n, drain, 0)
 
-    @pl.when(is_edge)
+    @pl.when(sends_far)
     def _():
         far_copy().wait_send()
 
@@ -643,16 +697,11 @@
             else:
                 aid_copy(index).wait_send()
 
-    for part in range(n):
-        pltpu.make_async_copy(
-            landed.at[part], out_ref.at[:, pl.ds(part * quarter, quarter)], store_sem.at[part]
-        ).wait()
-
 
 def chunk_ends(heads, groups):
     lent = max(1, round(heads * LENT_SHARE))
     kept = heads - lent
-    return [heads // 4, heads // 2, kept, heads]
+    return [heads // 8, heads * 3 // 8, heads * 5 // 8, kept, heads]
 
 
 def key_blocks_back(tokens, rows):
@@ -678,9 +727,9 @@
     bf16, f32, dma = jnp.bfloat16, jnp.float32, pltpu.SemaphoreType.DMA
     return pl.pallas_call(
         functools.partial(fused_kernel, n, groups, back),
-        out_shape=jax.ShapeDtypeStruct((rows, features), bf16),
+        out_shape=pltpu.VMEM((rows, features), bf16),
         in_specs=[any_space] * 6,
-        out_specs=any_space,
+        out_specs=pl.BlockSpec(memory_space=pltpu.VMEM),
         scratch_shapes=[
             pltpu.VMEM((rows, query_width), bf16),
             pltpu.VMEM((rows, kv_heads * HEAD_SIZE), bf16),
@@ -722,7 +771,6 @@
             dma,
             dma((n,)),
             dma((n,)),
-            dma((n,)),
         ],
         compiler_params=pltpu.CompilerParams(collective_id=0, has_side_effects=True),
     )(query_matrix, key_matrix, value_matrix, doc_ids.reshape(tokens // rows, rows), jnp.asarray(table), out_weight)

time: 53.6 us -> 49.7 us (0.927)
  Pallas kernels: 51.7 us -> 48.8 us
  local copies, waits for them, and re-layouts: 1.67 us -> 0.71 us
    pallas_call x1, Pallas kernels: 51.7 us -> 48.8 us  [fused(): pl.pallas_call(functools.partial(fused_kernel, n, groups, back), out_shap...]
    unnamed x1, local copies, waits for them, and re-layouts: 1.67 us -> 0.71 us
where the time goes in v3:
time: 49.7 us; the launch traced here: 49.5 us
  Pallas kernels  48.8 us (98%)
  local copies, waits for them, and re-layouts  0.71 us (1%)
    pallas_call x1, Pallas kernels, fused(): pl.pallas_call(functools.partial(fused_kernel, n, groups, back), out_shap...  48.8 us

profile of v3, /device:TPU:3, one launch (start us, length us, event | category | flops | bytes accessed | tf_op | source)
XLA Modules:
  0.0 49.5 jit_solution(3545877473797728494)
XLA Ops:
  0.0 48.8 %shard_map.64 = bf16[128,1024]{1,0:T(8,128)(2,1)S(1)} custom-call(bf16[128,2048]{1,0:T(8,128)(2,1)} %query_ref.1, bf16[128,256]{1,0:T(8,128)(2,1)} %key_ref.1, bf16[128,256]{1,0:T(8,128)(2,1)} %value_ref.1, s32[4,128]{1,0:T(4,128)} %bitcast.1, f32[2,512,128]{2,1,0:T(8,128)} %constant.2.clone.table_ref, bf16[2048,1024]{1,0:T(8,128)(2,1)} %weight_ref.1), custom_call_target="tpu_custom_call" | custom-call | tf_op jit(solution)/shard_map/pallas_call | solution.py:728
  48.8 0.7 %copy.8 = bf16[128,1024]{1,0:T(8,128)(2,1)} copy(bf16[128,1024]{1,0:T(8,128)(2,1)S(1)} %shard_map.64) | data formatting | bytes 524288

commit v4 on v3

--- a/solution.py
+++ b/solution.py
@@ -127,7 +127,7 @@
     quarter = partial.shape[3]
     last = n - 1
     lent_chunk = chunks - 1
-    pieces = lend_send.shape[0]
+    pieces = lend_recv.shape[0]
     half_rows = lent.shape[0] // groups
     piece_rows = half_rows // pieces
 
@@ -189,11 +189,11 @@
         )
         for head in range(kv_heads)
     ]
+    lent_start = starts[lent_chunk] * HEAD_SIZE
+    weight_rows = [pl.ds(lent_start, lent.shape[0]), pl.ds(0, lent_start)]
     weight_loads = [
-        pltpu.make_async_copy(
-            weight_ref.at[columns_of(chunk)], weight.at[columns_of(chunk)], weight_sem.at[chunk]
-        )
-        for chunk in [lent_chunk] + list(range(lent_chunk))
+        pltpu.make_async_copy(weight_ref.at[part], weight.at[part], weight_sem.at[index])
+        for index, part in enumerate(weight_rows)
     ]
     for load in loads + value_loads + weight_loads:
         load.start()
@@ -241,14 +241,14 @@
         start = pl.multiple_of(group * half_rows + piece * piece_rows, piece_rows)
         return remote(
             weight.at[pl.ds(starts[lent_chunk] * HEAD_SIZE + start, piece_rows)], lent.at[pl.ds(start, piece_rows)],
-            lend_send.at[piece], lend_recv.at[piece], jnp.where(ctx == 0, 1, last - 1), tp,
+            lend_send, lend_recv.at[piece], jnp.where(ctx == 0, 1, last - 1), tp,
         )
 
     def share_copy(piece, owner):
         start = pl.multiple_of(owner * half_rows + piece * piece_rows, piece_rows)
         here = lent.at[pl.ds(start, piece_rows)]
         return pltpu.make_async_remote_copy(
-            src_ref=here, dst_ref=here, send_sem=share_send.at[piece], recv_sem=share_recv.at[piece],
+            src_ref=here, dst_ref=here, send_sem=share_send, recv_sem=share_recv,
             device_id={"groups": other_group}, device_id_type=MESH,
         )
 
@@ -296,13 +296,13 @@
 
     def chunk_copy(block, chunk, send, to_ctx):
         here = gathered.at[block, :, columns_of(chunk)]
-        return remote(here, here, send.at[block, chunk], chunk_recv.at[block, chunk], to_ctx, tp)
+        return remote(here, here, send, chunk_recv.at[block, chunk], to_ctx, tp)
 
     def away_copy(block, chunk):
-        return chunk_copy(block, chunk, away_send, ctx + away)
+        return chunk_copy(block, chunk, away_send.at[jnp.where(block == ctx, 0, 1)], ctx + away)
 
     def edge_copy(block, chunk):
-        return chunk_copy(block, chunk, edge_send, helped)
+        return chunk_copy(block, chunk, edge_send.at[(block - ctx) * away], helped)
 
     scale = HEAD_SIZE ** (-0.5) * math.log2(math.e)
     contract = (((1,), (1,)), ((), ()))
@@ -352,12 +352,12 @@
     def pair_copy(place, index):
         return remote(
             partial.at[place, pair_across if index else pair], pair_in.at[place, index],
-            pair_send.at[place, index], pair_recv.at[place, index], ctx, pair,
+            pair_send, pair_recv.at[place, index], ctx, pair,
         )
 
     def cross_copy(place):
         return remote(
-            crossing.at[place], cross_in.at[place], cross_send.at[place], cross_recv.at[place], ctx, across
+            crossing.at[place], cross_in.at[place], cross_send, cross_recv.at[place], ctx, across
         )
 
     parts = (pair_across, pair, across, tp)
@@ -405,7 +405,7 @@
 
     def result_copy(block):
         return remote(
-            summed.at[block], landed.at[tp], result_send.at[block], result_recv.at[tp], block, ctx
+            summed.at[block], landed.at[tp], result_send.at[block], result_recv, block, ctx
         )
 
     def finish(block):
@@ -428,7 +428,7 @@
 
     def aid_copy(index):
         return remote(
-            summed.at[n + index], landed_aid.at[tp], result_send.at[n + index], aid_recv.at[tp],
+            summed.at[n + index], landed_aid.at[tp], result_send.at[n + index], aid_recv,
             block_at(index), helped,
         )
 
@@ -437,7 +437,7 @@
 
     def far_copy():
         return remote(
-            halves, landed_far.at[tp], half_send, far_recv.at[tp], far_block, ctx
+            halves, landed_far.at[tp], half_send, far_recv, far_block, ctx
         )
 
     def pair_sum(place, index):
@@ -504,8 +504,8 @@
         project(block_at(distance), chunk, distance, False)
 
     def aid_both():
-        for piece in range(pieces):
-            share_copy(piece, other_group).wait_recv()
+        arrived = lent.at[pl.ds(pl.multiple_of(other_group * half_rows, half_rows), half_rows)]
+        remote(arrived, arrived, share_send, share_recv, ctx, pair).wait_recv()
         aid(1)
         aid(0)
 
@@ -585,30 +585,35 @@
     gets_aid = ((tp == 0) | (tp == last)) & (ctx != tp)
     aid_here = is_helper & (tp == helped)
 
+    def landed_all(landing, recv, local):
+        if local is None:
+            return remote(landing, landing, half_send, recv, ctx, pair).wait_recv()
+
+        @pl.when(local)
+        def _():
+            some = landing.at[pl.ds(0, n - 1)]
+            remote(some, some, half_send, recv, ctx, pair).wait_recv()
+
+        @pl.when(jnp.logical_not(local))
+        def _():
+            remote(landing, landing, half_send, recv, ctx, pair).wait_recv()
+
     @pl.when(is_far)
     def _():
-        for part in range(n):
-            far = far_recv.at[part]
-            remote(halves, landed_far.at[part], half_send, far, ctx, part).wait_recv()
+        landed_all(landed_far, far_recv, None)
+
+    @pl.when(jnp.logical_not(is_far))
+    def _():
+        landed_all(landed, result_recv, tp == ctx)
 
     @pl.when(gets_aid)
     def _():
-        for part in range(n):
-            @pl.when(jnp.logical_not(aid_here & (tp == part)))
-            def _():
-                here = aid_recv.at[part]
-                remote(summed.at[n], landed_aid.at[part], result_send.at[n], here, ctx, part).wait_recv()
+        landed_all(landed_aid, aid_recv, aid_here)
 
     def both_halves(landing, part):
         return landing[part, 0].astype(jnp.float32) + landing[(part + 2) % n, 1].astype(jnp.float32)
 
     for part in range(n):
-        @pl.when(jnp.logical_not(is_far | ((tp == ctx) & (tp == part))))
-        def _():
-            remote(
-                summed.at[0], landed.at[part], result_send.at[0], result_recv.at[part], ctx, part
-            ).wait_recv()
-
         columns = pl.ds(part * quarter, quarter)
 
         @pl.when(is_far & jnp.logical_not(gets_aid))
@@ -643,33 +648,35 @@
         def _():
             kv_copy(back - 1, head).wait_send()
 
-    for piece in range(pieces):
-        @pl.when(is_edge)
-        def _():
-            lend_copy(piece).wait_send()
-
-        @pl.when(is_helper)
-        def _():
-            share_copy(piece, group).wait_send()
+    def sent(source, send):
+        remote(source, source, send, chunk_recv.at[0, 0], ctx, pair).wait_send()
+
+    half_lent = lent.at[pl.ds(0, half_rows)]
+    sent(gathered.at[ctx], away_send.at[0])
+
+    @pl.when(is_edge)
+    def _():
+        sent(half_lent, lend_send)
+        sent(pair_in.at[pl.ds(0, n)], pair_send)
+        sent(cross_in.at[pl.ds(0, n - 1)], cross_send)
+
+    @pl.when(is_helper)
+    def _():
+        sent(half_lent, share_send)
+        sent(gathered.at[helped], away_send.at[1])
+        sent(pair_in, pair_send)
+        for distance in range(n - 1):
+            sent(gathered.at[block_at(distance), :, pl.ds(0, starts[lent_chunk] * HEAD_SIZE)], edge_send.at[distance])
+
+    @pl.when(ctx == 1)
+    def _():
+        sent(cross_in, cross_send)
+
+    @pl.when(ctx == last - 1)
+    def _():
+        sent(cross_in.at[pl.ds(0, 2 * n - 2)], cross_send)
 
     def drain(block, carry):
-        for chunk in range(chunks):
-            @pl.when((block == ctx) | (is_helper & (block == helped)))
-            def _():
-                away_copy(block, chunk).wait_send()
-
-            if chunk < lent_chunk:
-                @pl.when(is_helper & (block != helped))
-                def _():
-                    edge_copy(block, chunk).wait_send()
-
-        for index in range(2):
-            pair_copy(block, index).wait_send()
-
-        @pl.when((block != far_block) | jnp.logical_not(sends_far))
-        def _():
-            cross_copy(block).wait_send()
-
         own_part = (block == ctx) & (tp == ctx)
 
         @pl.when(((block != far_block) | jnp.logical_not(sends_far)) & jnp.logical_not(own_part))
@@ -687,9 +694,6 @@
     @pl.when(is_helper)
     def _():
         for index in range(n - 1):
-            for side in range(2):
-                pair_copy(n + index, side).wait_send()
-            cross_copy(n + index).wait_send()
             if index == 0:
                 @pl.when(tp != helped)
                 def _():
@@ -752,25 +756,25 @@
             pltpu.VMEM((n, 2, rows, quarter), bf16),
             pltpu.VMEM((n, rows, quarter), bf16),
             dma((4 + kv_heads,)),
-            dma((chunks,)),
+            dma((2,)),
             dma((back + 1, kv_heads)),
-            dma((back + 1, kv_heads)),
+            dma((back, kv_heads)),
+            dma((2,)),
+            dma((n - 1,)),
             dma((n, chunks)),
-            dma((n, chunks)),
-            dma((n, chunks)),
+            dma,
             dma((pieces,)),
-            dma((pieces,)),
-            dma((pieces,)),
-            dma((pieces,)),
+            dma,
+            dma,
+            dma,
             dma((2 * n - 1, 2)),
-            dma((2 * n - 1, 2)),
+            dma,
             dma((2 * n - 1,)),
             dma((2 * n - 1,)),
-            dma((2 * n - 1,)),
-            dma((n,)),
             dma,
-            dma((n,)),
-            dma((n,)),
+            dma,
+            dma,
+            dma,
         ],
         compiler_params=pltpu.CompilerParams(collective_id=0, has_side_effects=True),
     )(query_matrix, key_matrix, value_matrix, doc_ids.reshape(tokens // rows, rows), jnp.asarray(table), out_weight)

time: 49.7 us -> 48.7 us (0.980)
  Pallas kernels: 48.8 us -> 47.8 us
    pallas_call x1, Pallas kernels: 48.8 us -> 47.8 us  [fused(): pl.pallas_call(functools.partial(fused_kernel, n, groups, back), out_shap...]
where the time goes in v4:
time: 48.7 us; the launch traced here: 48.6 us
  Pallas kernels  47.8 us (98%)
  local copies, waits for them, and re-layouts  0.71 us (1%)
    pallas_call x1, Pallas kernels, fused(): pl.pallas_call(functools.partial(fused_kernel, n, groups, back), out_shap...  47.8 us

profile of v4, /device:TPU:3, one launch (start us, length us, event | category | flops | bytes accessed | tf_op | source)
XLA Modules:
  0.0 48.6 jit_solution(3742751838996825159)
XLA Ops:
  0.0 47.8 %shard_map.64 = bf16[128,1024]{1,0:T(8,128)(2,1)S(1)} custom-call(bf16[128,2048]{1,0:T(8,128)(2,1)} %query_ref.1, bf16[128,256]{1,0:T(8,128)(2,1)} %key_ref.1, bf16[128,256]{1,0:T(8,128)(2,1)} %value_ref.1, s32[4,128]{1,0:T(4,128)} %bitcast.1, f32[2,512,128]{2,1,0:T(8,128)} %constant.2.clone.table_ref, bf16[2048,1024]{1,0:T(8,128)(2,1)} %weight_ref.1), custom_call_target="tpu_custom_call" | custom-call | tf_op jit(solution)/shard_map/pallas_call | solution.py:732
  47.9 0.7 %copy.8 = bf16[128,1024]{1,0:T(8,128)(2,1)} copy(bf16[128,1024]{1,0:T(8,128)(2,1)S(1)} %shard_map.64) | data formatting | bytes 524288

commit v5 on v4

--- a/solution.py
+++ b/solution.py
@@ -370,7 +370,7 @@
         if index < 2:
             pair_copy(place, 1 - index).start()
 
-    def project(block, chunk, keep, own):
+    def project(block, chunk, keep, final):
         for index, part in enumerate(parts):
             product = jnp.dot(
                 gathered[block, :, columns_of(chunk)], weight[columns_of(chunk), part_columns(part)],
@@ -378,16 +378,8 @@
             )
             if chunk > 0:
                 product = product + sums[keep, index]
-            if chunk == lent_chunk:
+            if chunk == final:
                 emit(block, index, product)
-            elif chunk == lent_chunk - 1 and not own:
-                @pl.when(is_edge)
-                def _():
-                    emit(block, index, product)
-
-                @pl.when(jnp.logical_not(is_edge))
-                def _():
-                    sums[keep, index] = product
             else:
                 sums[keep, index] = product
 
@@ -405,7 +397,7 @@
 
     def result_copy(block):
         return remote(
-            summed.at[block], landed.at[tp], result_send.at[block], result_recv, block, ctx
+            summed.at[block], landed.at[tp], result_send, result_recv, block, ctx
         )
 
     def finish(block):
@@ -424,20 +416,20 @@
     for load in weight_loads[1:]:
         load.wait()
     for chunk in range(chunks):
-        project(ctx, chunk, 0, True)
+        project(ctx, chunk, 0, lent_chunk)
 
     def aid_copy(index):
         return remote(
-            summed.at[n + index], landed_aid.at[tp], result_send.at[n + index], aid_recv,
+            summed.at[n + index], landed_aid.at[tp], result_send, aid_recv,
             block_at(index), helped,
         )
 
     far_block = jnp.where(ctx < n // 2, last, 0)
     sends_far = ctx != 1
 
-    def far_copy():
+    def far_copy(index):
         return remote(
-            halves, landed_far.at[tp], half_send, far_recv, far_block, ctx
+            halves.at[index], landed_far.at[tp, index], half_send, far_recv, far_block, ctx
         )
 
     def pair_sum(place, index):
@@ -449,7 +441,7 @@
     def finish_far():
         for index in (1, 0):
             halves[index] = pair_sum(far_block, index)
-        far_copy().start()
+            far_copy(index).start()
 
     def aid(index):
         for position, part in enumerate(parts):
@@ -487,7 +479,7 @@
                 if chunk == lent_chunk - 1:
                     finish(block_at(distance - 1))
                 take(block, chunk, None)
-                project(block, chunk, 1, False)
+                project(block, chunk, 1, lent_chunk - 1)
                 if chunk == 0:
                     cross(block_at(distance - 1))
             return carry
@@ -497,11 +489,11 @@
 
     def near(chunk):
         take(helped, chunk, away_copy)
-        project(helped, chunk, 0, False)
+        project(helped, chunk, 0, lent_chunk)
 
     def far(distance, chunk):
         take(block_at(distance), chunk, edge_copy if chunk < lent_chunk else None)
-        project(block_at(distance), chunk, distance, False)
+        project(block_at(distance), chunk, distance, lent_chunk)
 
     def aid_both():
         arrived = lent.at[pl.ds(pl.multiple_of(other_group * half_rows, half_rows), half_rows)]
@@ -676,30 +668,32 @@
     def _():
         sent(cross_in.at[pl.ds(0, 2 * n - 2)], cross_send)
 
-    def drain(block, carry):
-        own_part = (block == ctx) & (tp == ctx)
-
-        @pl.when(((block != far_block) | jnp.logical_not(sends_far)) & jnp.logical_not(own_part))
-        def _():
-            result_copy(block).wait_send()
-
-        return carry
-
-    lax.fori_loop(0, n, drain, 0)
+    def sent_results(count):
+        local = (tp == ctx) | (is_helper & (tp == helped))
+
+        @pl.when(local)
+        def _():
+            sent(summed.at[pl.ds(0, count - 1)], result_send)
+
+        @pl.when(jnp.logical_not(local))
+        def _():
+            sent(summed.at[pl.ds(0, count)], result_send)
+
+    @pl.when(is_edge)
+    def _():
+        sent_results(n - 1)
+
+    @pl.when(ctx == 1)
+    def _():
+        sent_results(2 * n - 1)
+
+    @pl.when(ctx == last - 1)
+    def _():
+        sent_results(2 * n - 2)
 
     @pl.when(sends_far)
     def _():
-        far_copy().wait_send()
-
-    @pl.when(is_helper)
-    def _():
-        for index in range(n - 1):
-            if index == 0:
-                @pl.when(tp != helped)
-                def _():
-                    aid_copy(0).wait_send()
-            else:
-                aid_copy(index).wait_send()
+        sent(halves, half_send)
 
 
 def chunk_ends(heads, groups):
@@ -770,7 +764,7 @@
             dma((2 * n - 1, 2)),
             dma,
             dma((2 * n - 1,)),
-            dma((2 * n - 1,)),
+            dma,
             dma,
             dma,
             dma,

time: 48.7 us -> 48.7 us (level)
  no operation moved by 1% of the time
where the time goes in v5:
time: 48.7 us; the launch traced here: 48.5 us
  Pallas kernels  47.8 us (98%)
  local copies, waits for them, and re-layouts  0.71 us (1%)
    pallas_call x1, Pallas kernels, fused(): pl.pallas_call(functools.partial(fused_kernel, n, groups, back), out_shap...  47.8 us

profile of v5, /device:TPU:3, one launch (start us, length us, event | category | flops | bytes accessed | tf_op | source)
XLA Modules:
  0.0 48.5 jit_solution(15653526976537281181)
XLA Ops:
  0.0 47.8 %shard_map.64 = bf16[128,1024]{1,0:T(8,128)(2,1)S(1)} custom-call(bf16[128,2048]{1,0:T(8,128)(2,1)} %query_ref.1, bf16[128,256]{1,0:T(8,128)(2,1)} %key_ref.1, bf16[128,256]{1,0:T(8,128)(2,1)} %value_ref.1, s32[4,128]{1,0:T(4,128)} %bitcast.1, f32[2,512,128]{2,1,0:T(8,128)} %constant.2.clone.table_ref, bf16[2048,1024]{1,0:T(8,128)(2,1)} %weight_ref.1), custom_call_target="tpu_custom_call" | custom-call | tf_op jit(solution)/shard_map/pallas_call | solution.py:726
  47.8 0.7 %copy.8 = bf16[128,1024]{1,0:T(8,128)(2,1)} copy(bf16[128,1024]{1,0:T(8,128)(2,1)S(1)} %shard_map.64) | data formatting | bytes 524288

commit v6 on v5

--- a/solution.py
+++ b/solution.py
@@ -699,7 +699,7 @@
 def chunk_ends(heads, groups):
     lent = max(1, round(heads * LENT_SHARE))
     kept = heads - lent
-    return [heads // 8, heads * 3 // 8, heads * 5 // 8, kept, heads]
+    return [heads * 3 // 16, heads * 7 // 16, heads * 11 // 16, kept, heads]
 
 
 def key_blocks_back(tokens, rows):

time: 48.7 us -> 48.5 us (level)
  no operation moved by 1% of the time
where the time goes in v6:
time: 48.5 us; the launch traced here: 48.4 us
  Pallas kernels  47.7 us (98%)
  local copies, waits for them, and re-layouts  0.71 us (1%)
    pallas_call x1, Pallas kernels, fused(): pl.pallas_call(functools.partial(fused_kernel, n, groups, back), out_shap...  47.7 us

profile of v6, /device:TPU:3, one launch (start us, length us, event | category | flops | bytes accessed | tf_op | source)
XLA Modules:
  0.0 48.4 jit_solution(14026623663507914684)
XLA Ops:
  0.0 47.7 %shard_map.64 = bf16[128,1024]{1,0:T(8,128)(2,1)S(1)} custom-call(bf16[128,2048]{1,0:T(8,128)(2,1)} %query_ref.1, bf16[128,256]{1,0:T(8,128)(2,1)} %key_ref.1, bf16[128,256]{1,0:T(8,128)(2,1)} %value_ref.1, s32[4,128]{1,0:T(4,128)} %bitcast.1, f32[2,512,128]{2,1,0:T(8,128)} %constant.2.clone.table_ref, bf16[2048,1024]{1,0:T(8,128)(2,1)} %weight_ref.1), custom_call_target="tpu_custom_call" | custom-call | tf_op jit(solution)/shard_map/pallas_call | solution.py:726
  47.7 0.7 %copy.8 = bf16[128,1024]{1,0:T(8,128)(2,1)} copy(bf16[128,1024]{1,0:T(8,128)(2,1)S(1)} %shard_map.64) | data formatting | bytes 524288
